TPU v7x, 32 devices: a whole 2x2x4 slice. The times are simulated.
32 devices in a mesh: grp: 2 (over y), seq: 8 (over z, x), tp: 2 (over core).
Axes of the slice: x: 2, y: 2, z: 4, core: 2. Of those that a mesh axis runs over, the one named last changes fastest.
Arguments:
- queries: bfloat16 [4096, 2048], P(('grp', 'seq'), 'tp'), parts along dimension 0, may hold values from -9 to 9
- keys: bfloat16 [4096, 2048], P(('grp', 'seq'), 'tp'), parts along dimension 0, may hold values from -9 to 9
- values: bfloat16 [4096, 2048], P(('grp', 'seq'), 'tp'), parts along dimension 0, may hold values from -18 to 18
- segment_ids: int32 [4096], P(('grp', 'seq')), parts along dimension 0, may hold values from 0 to 7, never falling along the last dimension, each value on 1 to 512 neighbouring positions
- modality: int32 [4096], P(('grp', 'seq')), parts along dimension 0, may hold values 0 or 1
- norm_gain: float32 [2, 2048], P(None, 'tp'), may hold values from 0.1 to 1.9
Outputs:
- blended: bfloat16 [4096, 2048], P(('grp', 'seq'), 'tp'), parts along dimension 0
There are 2 independent parts, one for each index of `grp`. A program takes and returns all parts, laid end to end along the dimension named above; an argument that names none is the same for every part. Nothing has to cross between parts.
Inputs may be any that keep to these rules, and one draw needn't show every extreme that they name: `segment_ids`: ids never fall along the sequence; each document holds 1 to 512 tokens, and one holds exactly that many.
All inputs are finite; a program needn't handle non-finite values. No bound on the sum of `modality` on one device may be relied on, other than what follows from the above.
Results may differ from a plain program's by a relative error of at most 0.009.
Values may be sent and summed in bfloat16 or wider, within the bound.
A program may use at most 64 MiB of HBM per device.

v0:
```python
import functools

import jax
import jax.numpy as jnp
from jax import lax
from jax.experimental import pallas as pl
from jax.experimental.pallas import tpu as pltpu
from jax.sharding import PartitionSpec as P

HEADS = 16
HEAD_DIM = 128
REACH = 2
MESH = pl.DeviceIdType.MESH
PIECES = 4
DIRECT = 2


def kernel(
    n,
    heads,
    rows,
    q_hbm,
    k_hbm,
    v_hbm,
    seg_ref,
    mod_ref,
    att,
    inverse_ref,
    image_ref,
    q_own,
    own,
    buf1,
    buf2,
    hop,
    seg1,
    seg2,
    bias,
    squares,
    mine,
    theirs,
    in_sem,
    send_a,
    send_b,
    send_c,
    recv_1,
    recv_2,
    hop_recv,
    seg_send,
    seg_recv,
    sq_sem,
):
    s = lax.axis_index("seq")
    t = lax.axis_index("tp")
    even = lax.rem(s, 2) == 0
    odd = lax.rem(s, 2) == 1
    has_next = s + 2 < n
    has_prev = s >= 2
    ahead = odd & (s + 1 < n)
    passes = even & has_next
    behind = even & has_prev
    pair = s + 1 - 2 * lax.rem(s, 2)

    half = PIECES // 2
    depth = rows // half

    def columns_of(h):
        return pl.ds(h * HEAD_DIM, HEAD_DIM)

    def load_piece(h, p):
        source = k_hbm if p < half else v_hbm
        piece = pl.ds((p % half) * depth, depth)
        return pltpu.make_async_copy(
            source.at[piece, columns_of(h)], own.at[h, p], in_sem.at[h, p]
        )

    def load_q(h):
        return pltpu.make_async_copy(q_hbm.at[:, columns_of(h)], q_own.at[h], in_sem.at[h, PIECES])

    last = heads - 1
    direct = range(PIECES - DIRECT, PIECES)
    for p in direct:
        load_piece(last, p).start()
    for h in range(heads):
        for p in range(PIECES):
            if h < last or p not in direct:
                load_piece(h, p).start()

    barrier = pltpu.get_barrier_semaphore()
    pl.semaphore_signal(barrier, inc=1, device_id={"tp": 1 - t}, device_id_type=MESH)
    pl.semaphore_signal(barrier, inc=1, device_id={"seq": pair}, device_id_type=MESH)

    @pl.when(has_next)
    def _():
        pl.semaphore_signal(barrier, inc=1, device_id={"seq": s + 2}, device_id_type=MESH)

    @pl.when(has_prev)
    def _():
        pl.semaphore_signal(barrier, inc=1, device_id={"seq": s - 2}, device_id_type=MESH)

    peers = 2 + jnp.where(has_next, 1, 0) + jnp.where(has_prev, 1, 0)
    pl.semaphore_wait(barrier, peers)

    def remote(source, target, send, recv, where):
        return pltpu.make_async_remote_copy(
            src_ref=source,
            dst_ref=target,
            send_sem=send,
            recv_sem=recv,
            device_id={"seq": where},
            device_id_type=MESH,
        )

    def flow_a(h, p):
        return remote(own.at[h, p], buf1.at[h, p], send_a.at[h, p], recv_1.at[h, p], pair)

    def flow_b(h, p):
        return remote(own.at[h, p], buf2.at[h, p], send_b.at[h, p], recv_2.at[h, p], s + 2)

    def flow_c(h, p):
        return remote(buf2.at[h, p], buf1.at[h, p], send_c.at[h, p], recv_1.at[h, p], pair)

    def flow_d(p):
        i = p - direct[0]
        return remote(own.at[last, p], hop.at[i], send_c.at[last, p], hop_recv.at[i], pair)

    def flow_e(p):
        i = p - direct[0]
        return remote(hop.at[i], buf1.at[last, p], send_c.at[last, p], recv_1.at[last, p], s + 2)

    def forwards(h, p):
        return odd & has_prev & (h < last) if p in direct else odd & has_prev

    def seg_a():
        return remote(seg_ref, seg1, seg_send.at[0], seg_recv.at[0], pair)

    def seg_b():
        return remote(seg_ref, seg2, seg_send.at[1], seg_recv.at[1], s + 2)

    def seg_c():
        return remote(seg2, seg1, seg_send.at[2], seg_recv.at[0], pair)

    @pl.when(even)
    def _():
        seg_a().start()

    @pl.when(has_next)
    def _():
        seg_b().start()

    for p in direct:
        load_piece(last, p).wait()

        @pl.when(ahead)
        def _():
            flow_d(p).start()

    def send_pieces(h, waits):
        for p in range(PIECES):
            if p in waits:
                load_piece(h, p).wait()

            @pl.when(has_next)
            def _():
                flow_b(h, p).start()

            @pl.when(even)
            def _():
                flow_a(h, p).start()

        load_q(h).start()

    def send(h, carry):
        send_pieces(h, range(PIECES))
        return carry

    lax.fori_loop(0, last, send, 0)
    send_pieces(last, range(PIECES - DIRECT))

    @pl.when(s < 1)
    def _():
        buf1[...] = jnp.zeros_like(buf1)
        seg1[...] = jnp.full_like(seg1, -1)

    @pl.when(s < 2)
    def _():
        buf2[...] = jnp.zeros_like(buf2)
        seg2[...] = jnp.full_like(seg2, -1)

    def column(row):
        return jnp.transpose(jnp.broadcast_to(row, (HEAD_DIM, rows)))

    query_seg = column(seg_ref[...])[:, :1]
    query_pos = lax.broadcasted_iota(jnp.int32, (rows, rows), 0)
    key_pos = lax.broadcasted_iota(jnp.int32, (rows, rows), 1)
    allowed = (query_seg == seg_ref[...]) & (key_pos <= query_pos)
    bias[:, :rows] = jnp.where(allowed, 0.0, -jnp.inf)
    squares[...] = jnp.zeros_like(squares)
    image_ref[...] = column(mod_ref[...])

    @pl.when(has_prev)
    def _():
        seg_b().wait_recv()

    @pl.when(odd & has_prev)
    def _():
        seg_c().start()

    @pl.when(s >= 1)
    def _():
        seg_a().wait_recv()

    bias[:, rows : 2 * rows] = jnp.where(query_seg == seg1[...], 0.0, -jnp.inf)
    bias[:, 2 * rows :] = jnp.where(query_seg == seg2[...], 0.0, -jnp.inf)

    for p in direct:

        @pl.when(passes)
        def _():
            flow_d(p).wait_recv()
            flow_e(p).start()

    def scores_of(query, key):
        return lax.dot_general(
            query, key, (((1,), (1,)), ((), ())), preferred_element_type=jnp.float32
        )

    def arrive(h, pieces):
        for p in pieces:

            @pl.when(s >= 1)
            def _():
                flow_a(h, p).wait_recv()

    def head(h, carry):
        load_q(h).wait()
        query = q_own[h]
        scale = HEAD_DIM ** (-0.5)

        def scores_with(block, i):
            key = block[h, :half].reshape(rows, HEAD_DIM)
            return scores_of(query, key) * scale + bias[:, i * rows : (i + 1) * rows]

        def product(weight, block):
            value = block[h, half:].reshape(rows, HEAD_DIM)
            return jnp.dot(
                weight.astype(jnp.bfloat16), value, preferred_element_type=jnp.float32
            )

        for p in range(half):

            @pl.when(has_prev)
            def _():
                flow_b(h, p).wait_recv()

            @pl.when(forwards(h, p))
            def _():
                flow_c(h, p).start()

        @pl.when(odd & has_prev)
        def _():
            for p in range(half, PIECES):
                flow_b(h, p).wait_recv()

                @pl.when(forwards(h, p))
                def _():
                    flow_c(h, p).start()

        near = scores_with(own, 0)
        far = scores_with(buf2, 2)
        arrive(h, range(half))
        middle = scores_with(buf1, 1)
        top = jnp.max(jnp.maximum(jnp.maximum(near, middle), far), axis=1, keepdims=True)
        near = jnp.exp(near - top)
        far = jnp.exp(far - top)
        middle = jnp.exp(middle - top)
        total = jnp.sum(near + middle + far, axis=1, keepdims=True)
        acc = product(near, own)

        @pl.when(behind)
        def _():
            for p in range(half, PIECES):
                flow_b(h, p).wait_recv()

        arrive(h, range(half, PIECES))
        acc = acc + product(far, buf2) + product(middle, buf1)
        attended = (acc * (1.0 / total)).astype(jnp.bfloat16)
        att[h] = attended
        wide = attended.astype(jnp.float32)
        squares[...] += wide * wide
        return carry

    lax.fori_loop(0, heads, head, 0)

    partial = jnp.sum(squares[...], axis=1, keepdims=True)
    mine[...] = jnp.broadcast_to(partial, mine.shape)
    swap = pltpu.make_async_remote_copy(
        src_ref=mine,
        dst_ref=theirs,
        send_sem=sq_sem.at[0],
        recv_sem=sq_sem.at[1],
        device_id={"tp": 1 - t},
        device_id_type=MESH,
    )
    swap.start()
    swap.wait_recv()
    mean_square = (mine[...] + theirs[...]) / (HEADS * HEAD_DIM)
    inverse_ref[...] = lax.rsqrt(mean_square + 1e-05)
    swap.wait_send()

    for p in direct:

        @pl.when(ahead)
        def _():
            flow_d(p).wait_send()

        @pl.when(passes)
        def _():
            flow_e(p).wait_send()

    @pl.when(even)
    def _():
        seg_a().wait_send()

    @pl.when(has_next)
    def _():
        seg_b().wait_send()

    @pl.when(odd & has_prev)
    def _():
        seg_c().wait_send()

    def drain(h, carry):
        for p in range(PIECES):

            @pl.when(even)
            def _():
                flow_a(h, p).wait_send()

            @pl.when(has_next)
            def _():
                flow_b(h, p).wait_send()

            @pl.when(forwards(h, p))
            def _():
                flow_c(h, p).wait_send()

        return carry

    lax.fori_loop(0, heads, drain, 0)


def blend(heads, att, inverse_ref, image_ref, gain_ref, out_hbm, staged, out_sem):
    inverse = inverse_ref[...]
    image = image_ref[...] == 1
    copies = []
    for h in range(heads):
        columns = slice(h * HEAD_DIM, (h + 1) * HEAD_DIM)
        gain = jnp.where(image, gain_ref[1:2, columns], gain_ref[0:1, columns])
        staged[h] = (att[h].astype(jnp.float32) * inverse * gain).astype(staged.dtype)
        copy = pltpu.make_async_copy(
            staged.at[h], out_hbm.at[:, pl.ds(h * HEAD_DIM, HEAD_DIM)], out_sem.at[h]
        )
        copy.start()
        copies.append(copy)
    for copy in copies:
        copy.wait()


def on_device(n, queries, keys, values, segment_ids, modality, norm_gain):
    rows, width = queries.shape
    heads = width // HEAD_DIM
    vmem = pl.BlockSpec(memory_space=pltpu.VMEM)
    hbm = pl.BlockSpec(memory_space=pltpu.HBM)
    depth = 2 * rows // PIECES
    block = pltpu.VMEM((heads, PIECES, depth, HEAD_DIM), jnp.bfloat16)
    flow = pltpu.SemaphoreType.DMA((heads, PIECES))
    att, inverse, image = pl.pallas_call(
        functools.partial(kernel, n, heads, rows),
        out_shape=(
            pltpu.VMEM((heads, rows, HEAD_DIM), jnp.bfloat16),
            pltpu.VMEM((rows, HEAD_DIM), jnp.float32),
            pltpu.VMEM((rows, HEAD_DIM), jnp.int32),
        ),
        in_specs=[hbm, hbm, hbm, vmem, vmem],
        out_specs=(vmem, vmem, vmem),
        scratch_shapes=[
            pltpu.VMEM((heads, rows, HEAD_DIM), jnp.bfloat16),
            block,
            block,
            block,
            pltpu.VMEM((DIRECT, depth, HEAD_DIM), jnp.bfloat16),
            pltpu.VMEM((1, rows), jnp.int32),
            pltpu.VMEM((1, rows), jnp.int32),
            pltpu.VMEM((rows, (REACH + 1) * rows), jnp.float32),
            pltpu.VMEM((rows, HEAD_DIM), jnp.float32),
            pltpu.VMEM((rows, HEAD_DIM), jnp.float32),
            pltpu.VMEM((rows, HEAD_DIM), jnp.float32),
            pltpu.SemaphoreType.DMA((heads, PIECES + 1)),
            flow,
            flow,
            flow,
            flow,
            flow,
            pltpu.SemaphoreType.DMA((DIRECT,)),
            pltpu.SemaphoreType.DMA((3,)),
            pltpu.SemaphoreType.DMA((2,)),
            pltpu.SemaphoreType.DMA((2,)),
        ],
        compiler_params=pltpu.CompilerParams(
            collective_id=0, has_side_effects=True
        ),
    )(queries, keys, values, segment_ids.reshape(1, rows), modality.reshape(1, rows))
    return pl.pallas_call(
        functools.partial(blend, heads),
        out_shape=jax.ShapeDtypeStruct((rows, width), jnp.bfloat16),
        in_specs=[vmem, vmem, vmem, vmem],
        out_specs=hbm,
        scratch_shapes=[
            pltpu.VMEM((heads, rows, HEAD_DIM), jnp.bfloat16),
            pltpu.SemaphoreType.DMA((heads,)),
        ],
        compiler_params=pltpu.CompilerParams(vmem_limit_bytes=8 * 2**20),
    )(att, inverse, image, norm_gain)


def solution(mesh):
    return jax.shard_map(
        functools.partial(on_device, mesh.shape["seq"]),
        mesh=mesh,
        in_specs=(
            P(("grp", "seq"), "tp"),
            P(("grp", "seq"), "tp"),
            P(("grp", "seq"), "tp"),
            P(("grp", "seq")),
            P(("grp", "seq")),
            P(None, "tp"),
        ),
        out_specs=P(("grp", "seq"), "tp"),
        check_vma=False,
    )
```

profile of v0, /device:TPU:9, one launch (start us, length us, event | category | flops | bytes accessed | tf_op | source)
XLA Modules:
  0.0 34.0 jit_solution(9111891491565109210)
XLA Ops:
  0.0 0.0 copy-start
  0.0 33.1 %shard_map.64 = (bf16[8,256,128]{2,1,0:T(8,128)(2,1)S(1)}, f32[256,128]{1,0:T(8,128)S(1)}, s32[256,128]{1,0:T(8,128)S(1)}) custom-call(bf16[256,1024]{1,0:T(8,128)(2,1)} %q_hbm.1, bf16[256,1024]{1,0:T(8,128)(2,1)} %k_hbm.1, bf16[256,1024]{1,0:T(8,128)(2,1)} %v_hbm.1, s32[1,256]{1,0:T(1,128)} %bitcast.2, s32[1,256]{1,0:T(1,128)} %bitcast.3), custom_call_target="tpu_custom_call" | custom-call | tf_op jit(solution)/shard_map/pallas_call | solution.py:377
  33.1 0.0 copy-done
  33.1 0.9 %shard_map.65 = bf16[256,1024]{1,0:T(8,128)(2,1)} custom-call(bf16[8,256,128]{2,1,0:T(8,128)(2,1)S(1)} %get-tuple-element.8.att, f32[256,128]{1,0:T(8,128)S(1)} %get-tuple-element.9.inverse_ref, s32[256,128]{1,0:T(8,128)S(1)} %get-tuple-element.10.image_ref, f32[2,1024]{1,0:T(2,128)S(1)} %copy-done), custom_call_target="tpu_custom_call" | custom-call | tf_op jit(solution)/shard_map/pallas_call | solution.py:413
Async XLA Ops:
  0.0 33.1 %copy-start = (f32[2,1024]{1,0:T(2,128)S(1)}, f32[2,1024]{1,0:T(2,128)}, u32[]{:S(2)}) copy-start(f32[2,1024]{1,0:T(2,128)} %gain_ref.1) | copy-start | bytes 24580
where the time goes:
time: 34.2 us; the launch traced here: 34 us
  Pallas kernels  34 us (99%)
    pallas_call x1, Pallas kernels, on_device(): pl.pallas_call(functools.partial(kernel, n, heads, rows), out_shape=(pltp...  33.1 us
    pallas_call x1, Pallas kernels, on_device(): pl.pallas_call(functools.partial(blend, heads), out_shape=jax.ShapeDtypeS...  0.88 us

commit v1 on v0

--- a/solution.py
+++ b/solution.py
@@ -12,7 +12,8 @@
 REACH = 2
 MESH = pl.DeviceIdType.MESH
 PIECES = 4
-DIRECT = 2
+DIRECT = (2, 2)
+RELAY = 1
 
 
 def kernel(
@@ -22,8 +23,8 @@
     q_hbm,
     k_hbm,
     v_hbm,
-    seg_ref,
-    mod_ref,
+    seg_hbm,
+    mod_hbm,
     att,
     inverse_ref,
     image_ref,
@@ -32,6 +33,8 @@
     buf1,
     buf2,
     hop,
+    seg_ref,
+    mod_ref,
     seg1,
     seg2,
     bias,
@@ -44,7 +47,9 @@
     send_c,
     recv_1,
     recv_2,
+    hop_send,
     hop_recv,
+    id_sem,
     seg_send,
     seg_recv,
     sq_sem,
@@ -56,7 +61,7 @@
     has_next = s + 2 < n
     has_prev = s >= 2
     ahead = odd & (s + 1 < n)
-    passes = even & has_next
+    passes = even & has_next & (t == RELAY)
     behind = even & has_prev
     pair = s + 1 - 2 * lax.rem(s, 2)
 
@@ -77,58 +82,104 @@
         return pltpu.make_async_copy(q_hbm.at[:, columns_of(h)], q_own.at[h], in_sem.at[h, PIECES])
 
     last = heads - 1
-    direct = range(PIECES - DIRECT, PIECES)
-    for p in direct:
+    count = jnp.where(t == 0, DIRECT[0], DIRECT[1])
+    most = max(DIRECT)
+    tail = range(PIECES - most, PIECES)
+    relay = t == RELAY
+
+    def is_direct(p):
+        return p >= PIECES - count
+
+    def load_ids(i):
+        source, target = ((seg_hbm, seg_ref), (mod_hbm, mod_ref))[i]
+        return pltpu.make_async_copy(source, target, id_sem.at[i])
+
+    barrier = pltpu.get_barrier_semaphore()
+    across = (odd & ~relay & (s + 1 < n)) | (even & relay & has_next)
+    onward = even & relay & has_next
+    inward = even & ~relay & has_prev
+    peers = (
+        (None, {"tp": 1 - t}),
+        (None, {"seq": pair}),
+        (has_next, {"seq": s + 2}),
+        (has_prev, {"seq": s - 2}),
+        (across, {"seq": pair, "tp": 1 - t}),
+        (onward, {"seq": s + 2, "tp": 1 - t}),
+        (inward, {"seq": s - 2, "tp": 1 - t}),
+    )
+    expected = 0
+    for condition, peer in peers:
+
+        def greet(peer=peer):
+            pl.semaphore_signal(barrier, inc=1, device_id=peer, device_id_type=MESH)
+
+        if condition is None:
+            greet()
+            expected = expected + 1
+        else:
+            pl.when(condition)(greet)
+            expected = expected + jnp.where(condition, 1, 0)
+
+    for p in tail:
         load_piece(last, p).start()
+    load_ids(0).start()
     for h in range(heads):
         for p in range(PIECES):
-            if h < last or p not in direct:
+            if h < last or p not in tail:
                 load_piece(h, p).start()
-
-    barrier = pltpu.get_barrier_semaphore()
-    pl.semaphore_signal(barrier, inc=1, device_id={"tp": 1 - t}, device_id_type=MESH)
-    pl.semaphore_signal(barrier, inc=1, device_id={"seq": pair}, device_id_type=MESH)
-
-    @pl.when(has_next)
-    def _():
-        pl.semaphore_signal(barrier, inc=1, device_id={"seq": s + 2}, device_id_type=MESH)
-
-    @pl.when(has_prev)
-    def _():
-        pl.semaphore_signal(barrier, inc=1, device_id={"seq": s - 2}, device_id_type=MESH)
-
-    peers = 2 + jnp.where(has_next, 1, 0) + jnp.where(has_prev, 1, 0)
-    pl.semaphore_wait(barrier, peers)
-
-    def remote(source, target, send, recv, where):
+    load_ids(1).start()
+    load_ids(0).wait()
+    pl.semaphore_wait(barrier, expected)
+
+    def remote(source, target, send, recv, where, core=t):
         return pltpu.make_async_remote_copy(
             src_ref=source,
             dst_ref=target,
             send_sem=send,
             recv_sem=recv,
-            device_id={"seq": where},
+            device_id={"seq": where, "tp": core},
             device_id_type=MESH,
         )
 
     def flow_a(h, p):
-        return remote(own.at[h, p], buf1.at[h, p], send_a.at[h, p], recv_1.at[h, p], pair)
+        return remote(own.at[h, p], buf1.at[h, p], send_a, recv_1.at[h, p], pair)
 
     def flow_b(h, p):
-        return remote(own.at[h, p], buf2.at[h, p], send_b.at[h, p], recv_2.at[h, p], s + 2)
+        return remote(own.at[h, p], buf2.at[h, p], send_b, recv_2.at[h, p], s + 2)
 
     def flow_c(h, p):
-        return remote(buf2.at[h, p], buf1.at[h, p], send_c.at[h, p], recv_1.at[h, p], pair)
+        return remote(buf2.at[h, p], buf1.at[h, p], send_c.at[h], recv_1.at[h, p], pair)
 
     def flow_d(p):
-        i = p - direct[0]
-        return remote(own.at[last, p], hop.at[i], send_c.at[last, p], hop_recv.at[i], pair)
-
-    def flow_e(p):
-        i = p - direct[0]
-        return remote(hop.at[i], buf1.at[last, p], send_c.at[last, p], recv_1.at[last, p], s + 2)
+        i = p - tail[0]
+        return remote(
+            own.at[last, p], hop.at[t, i], hop_send.at[t, i], hop_recv.at[t, i], pair, RELAY
+        )
+
+    def flow_e(p, core):
+        i = p - tail[0]
+        return remote(
+            hop.at[core, i],
+            buf1.at[last, p],
+            hop_send.at[core, i],
+            recv_1.at[last, p],
+            s + 2,
+            core,
+        )
+
+    def hop_in(p, core):
+        i = p - tail[0]
+        return remote(
+            own.at[last, p], hop.at[core, i], hop_send.at[core, i], hop_recv.at[core, i], pair
+        )
+
+    def direct_of(core):
+        return range(PIECES - DIRECT[core], PIECES)
 
     def forwards(h, p):
-        return odd & has_prev & (h < last) if p in direct else odd & has_prev
+        if p not in tail:
+            return odd & has_prev
+        return odd & has_prev & ((h < last) | ~is_direct(p))
 
     def seg_a():
         return remote(seg_ref, seg1, seg_send.at[0], seg_recv.at[0], pair)
@@ -147,10 +198,10 @@
     def _():
         seg_b().start()
 
-    for p in direct:
+    for p in tail:
         load_piece(last, p).wait()
 
-        @pl.when(ahead)
+        @pl.when(ahead & is_direct(p))
         def _():
             flow_d(p).start()
 
@@ -174,7 +225,8 @@
         return carry
 
     lax.fori_loop(0, last, send, 0)
-    send_pieces(last, range(PIECES - DIRECT))
+    send_pieces(last, range(PIECES - most))
+    load_ids(1).wait()
 
     @pl.when(s < 1)
     def _():
@@ -212,12 +264,12 @@
     bias[:, rows : 2 * rows] = jnp.where(query_seg == seg1[...], 0.0, -jnp.inf)
     bias[:, 2 * rows :] = jnp.where(query_seg == seg2[...], 0.0, -jnp.inf)
 
-    for p in direct:
-
-        @pl.when(passes)
-        def _():
-            flow_d(p).wait_recv()
-            flow_e(p).start()
+    @pl.when(passes)
+    def _():
+        for core in (0, 1):
+            for p in direct_of(core):
+                hop_in(p, core).wait_recv()
+                flow_e(p, core).start()
 
     def scores_of(query, key):
         return lax.dot_general(
@@ -231,7 +283,7 @@
             def _():
                 flow_a(h, p).wait_recv()
 
-    def head(h, carry):
+    def head(h, pieces_apart):
         load_q(h).wait()
         query = q_own[h]
         scale = HEAD_DIM ** (-0.5)
@@ -281,17 +333,29 @@
             for p in range(half, PIECES):
                 flow_b(h, p).wait_recv()
 
-        arrive(h, range(half, PIECES))
-        acc = acc + product(far, buf2) + product(middle, buf1)
-        attended = (acc * (1.0 / total)).astype(jnp.bfloat16)
+        if pieces_apart:
+            acc = acc + product(far, buf2)
+            inverse = 1.0 / total
+            middle = middle.astype(jnp.bfloat16)
+            for p in range(half, PIECES):
+                arrive(h, (p,))
+                part = middle[:, (p - half) * depth : (p - half + 1) * depth]
+                acc = acc + jnp.dot(part, buf1[h, p], preferred_element_type=jnp.float32)
+            attended = (acc * inverse).astype(jnp.bfloat16)
+        else:
+            arrive(h, range(half, PIECES))
+            acc = acc + product(far, buf2) + product(middle, buf1)
+            attended = (acc * (1.0 / total)).astype(jnp.bfloat16)
         att[h] = attended
         wide = attended.astype(jnp.float32)
-        squares[...] += wide * wide
+        return wide * wide
+
+    def one(h, carry):
+        squares[...] += head(h, False)
         return carry
 
-    lax.fori_loop(0, heads, head, 0)
-
-    partial = jnp.sum(squares[...], axis=1, keepdims=True)
+    lax.fori_loop(0, last, one, 0)
+    partial = jnp.sum(squares[...] + head(last, True), axis=1, keepdims=True)
     mine[...] = jnp.broadcast_to(partial, mine.shape)
     swap = pltpu.make_async_remote_copy(
         src_ref=mine,
@@ -302,51 +366,45 @@
         device_id_type=MESH,
     )
     swap.start()
+
+    for p in tail:
+
+        @pl.when(ahead & is_direct(p))
+        def _():
+            flow_d(p).wait_send()
+
+    @pl.when(passes)
+    def _():
+        for core in (0, 1):
+            for p in direct_of(core):
+                flow_e(p, core).wait_send()
+
+    @pl.when(even)
+    def _():
+        seg_a().wait_send()
+        remote(own, own, send_a, recv_1.at[0, 0], pair).wait_send()
+
+    @pl.when(has_next)
+    def _():
+        seg_b().wait_send()
+        remote(own, own, send_b, recv_1.at[0, 0], pair).wait_send()
+
+    @pl.when(odd & has_prev)
+    def _():
+        seg_c().wait_send()
+        for h in range(last):
+            remote(buf2.at[h], buf1.at[h], send_c.at[h], recv_1.at[h, 0], pair).wait_send()
+
+    for p in range(PIECES):
+
+        @pl.when(forwards(last, p))
+        def _():
+            flow_c(last, p).wait_send()
+
     swap.wait_recv()
     mean_square = (mine[...] + theirs[...]) / (HEADS * HEAD_DIM)
     inverse_ref[...] = lax.rsqrt(mean_square + 1e-05)
     swap.wait_send()
-
-    for p in direct:
-
-        @pl.when(ahead)
-        def _():
-            flow_d(p).wait_send()
-
-        @pl.when(passes)
-        def _():
-            flow_e(p).wait_send()
-
-    @pl.when(even)
-    def _():
-        seg_a().wait_send()
-
-    @pl.when(has_next)
-    def _():
-        seg_b().wait_send()
-
-    @pl.when(odd & has_prev)
-    def _():
-        seg_c().wait_send()
-
-    def drain(h, carry):
-        for p in range(PIECES):
-
-            @pl.when(even)
-            def _():
-                flow_a(h, p).wait_send()
-
-            @pl.when(has_next)
-            def _():
-                flow_b(h, p).wait_send()
-
-            @pl.when(forwards(h, p))
-            def _():
-                flow_c(h, p).wait_send()
-
-        return carry
-
-    lax.fori_loop(0, heads, drain, 0)
 
 
 def blend(heads, att, inverse_ref, image_ref, gain_ref, out_hbm, staged, out_sem):
@@ -381,14 +439,16 @@
             pltpu.VMEM((rows, HEAD_DIM), jnp.float32),
             pltpu.VMEM((rows, HEAD_DIM), jnp.int32),
         ),
-        in_specs=[hbm, hbm, hbm, vmem, vmem],
+        in_specs=[hbm, hbm, hbm, hbm, hbm],
         out_specs=(vmem, vmem, vmem),
         scratch_shapes=[
             pltpu.VMEM((heads, rows, HEAD_DIM), jnp.bfloat16),
             block,
             block,
             block,
-            pltpu.VMEM((DIRECT, depth, HEAD_DIM), jnp.bfloat16),
+            pltpu.VMEM((2, max(DIRECT), depth, HEAD_DIM), jnp.bfloat16),
+            pltpu.VMEM((1, rows), jnp.int32),
+            pltpu.VMEM((1, rows), jnp.int32),
             pltpu.VMEM((1, rows), jnp.int32),
             pltpu.VMEM((1, rows), jnp.int32),
             pltpu.VMEM((rows, (REACH + 1) * rows), jnp.float32),
@@ -396,12 +456,14 @@
             pltpu.VMEM((rows, HEAD_DIM), jnp.float32),
             pltpu.VMEM((rows, HEAD_DIM), jnp.float32),
             pltpu.SemaphoreType.DMA((heads, PIECES + 1)),
+            pltpu.SemaphoreType.DMA,
+            pltpu.SemaphoreType.DMA,
+            pltpu.SemaphoreType.DMA((heads,)),
             flow,
             flow,
-            flow,
-            flow,
-            flow,
-            pltpu.SemaphoreType.DMA((DIRECT,)),
+            pltpu.SemaphoreType.DMA((2, max(DIRECT))),
+            pltpu.SemaphoreType.DMA((2, max(DIRECT))),
+            pltpu.SemaphoreType.DMA((2,)),
             pltpu.SemaphoreType.DMA((3,)),
             pltpu.SemaphoreType.DMA((2,)),
             pltpu.SemaphoreType.DMA((2,)),

time: 34.2 us -> 32.7 us (0.956)
  Pallas kernels: 34 us -> 32.5 us
    pallas_call x1, Pallas kernels: 33.1 us -> 31.6 us  [on_device(): pl.pallas_call(functools.partial(kernel, n, heads, rows), out_shape=(pltp...]
where the time goes in v1:
time: 32.7 us; the launch traced here: 32.5 us
  Pallas kernels  32.5 us (99%)
    pallas_call x1, Pallas kernels, on_device(): pl.pallas_call(functools.partial(kernel, n, heads, rows), out_shape=(pltp...  31.6 us
    pallas_call x1, Pallas kernels, on_device(): pl.pallas_call(functools.partial(blend, heads), out_shape=jax.ShapeDtypeS...  0.88 us

profile of v1, /device:TPU:9, one launch (start us, length us, event | category | flops | bytes accessed | tf_op | source)
XLA Modules:
  0.0 32.5 jit_solution(10814451775428507371)
XLA Ops:
  0.0 0.0 copy-start
  0.0 31.6 %shard_map.64 = (bf16[8,256,128]{2,1,0:T(8,128)(2,1)S(1)}, f32[256,128]{1,0:T(8,128)S(1)}, s32[256,128]{1,0:T(8,128)S(1)}) custom-call(bf16[256,1024]{1,0:T(8,128)(2,1)} %q_hbm.1, bf16[256,1024]{1,0:T(8,128)(2,1)} %k_hbm.1, bf16[256,1024]{1,0:T(8,128)(2,1)} %v_hbm.1, s32[1,256]{1,0:T(1,128)} %bitcast.2, s32[1,256]{1,0:T(1,128)} %bitcast.3), custom_call_target="tpu_custom_call" | custom-call | tf_op jit(solution)/shard_map/pallas_call | solution.py:435
  31.6 0.0 copy-done
  31.6 0.9 %shard_map.65 = bf16[256,1024]{1,0:T(8,128)(2,1)} custom-call(bf16[8,256,128]{2,1,0:T(8,128)(2,1)S(1)} %get-tuple-element.8.att, f32[256,128]{1,0:T(8,128)S(1)} %get-tuple-element.9.inverse_ref, s32[256,128]{1,0:T(8,128)S(1)} %get-tuple-element.10.image_ref, f32[2,1024]{1,0:T(2,128)S(1)} %copy-done), custom_call_target="tpu_custom_call" | custom-call | tf_op jit(solution)/shard_map/pallas_call | solution.py:475
Async XLA Ops:
  0.0 31.6 %copy-start = (f32[2,1024]{1,0:T(2,128)S(1)}, f32[2,1024]{1,0:T(2,128)}, u32[]{:S(2)}) copy-start(f32[2,1024]{1,0:T(2,128)} %gain_ref.1) | copy-start | bytes 24580

commit v2 on v1

v2 whole, which is shorter than its diff:
```python
import functools

import jax
import jax.numpy as jnp
from jax import lax
from jax.experimental import pallas as pl
from jax.experimental.pallas import tpu as pltpu
from jax.sharding import PartitionSpec as P

HEADS = 16
HEAD_DIM = 128
REACH = 2
MESH = pl.DeviceIdType.MESH
PIECES = 2
DIRECT = 1
QUERY = 3
NEVER = -1e30
RELAY = 1


def kernel(
    n,
    heads,
    rows,
    q_hbm,
    k_hbm,
    v_hbm,
    seg_hbm,
    mod_hbm,
    att,
    inverse_ref,
    image_ref,
    q_own,
    own,
    buf1,
    buf2,
    hop,
    q_next,
    part_out,
    lse_out,
    part_in,
    lse_in,
    seg_ref,
    mod_ref,
    seg1,
    seg2,
    seg_next,
    bias,
    bias_next,
    squares,
    mine,
    theirs,
    own_sem,
    q_sem,
    send_a,
    send_b,
    send_c,
    recv_1,
    recv_2,
    hop_send,
    hop_recv,
    ask_sem,
    part_sem,
    lse_sem,
    id_sem,
    seg_send,
    seg_recv,
    sq_sem,
):
    s = lax.axis_index("seq")
    t = lax.axis_index("tp")
    even = lax.rem(s, 2) == 0
    odd = lax.rem(s, 2) == 1
    has_next = s + 2 < n
    has_prev = s >= 2
    ahead = odd & (s + 1 < n)
    behind = even & has_prev
    asks = even & has_prev
    answers = even & has_next
    pair = s + 1 - 2 * lax.rem(s, 2)

    half = PIECES // 2
    depth = rows // half
    last = heads - 1
    kept = heads - QUERY
    shipped = range(kept, heads)
    cuts = n // 2 - 1
    scale = HEAD_DIM ** (-0.5)

    def direct_into(block):
        return DIRECT + 0 * block

    leaving = jnp.where(ahead, direct_into(s + 1), 0)
    passing = jnp.where(even & has_next, direct_into(s + 2), 0)
    arriving = jnp.where(asks, direct_into(s), 0)
    beside = heads - jnp.where(odd & has_prev, direct_into(s - 1), 0)

    def columns_of(h):
        return pl.ds(h * HEAD_DIM, HEAD_DIM)

    def load_piece(h, p):
        source = k_hbm if p < half else v_hbm
        piece = pl.ds((p % half) * depth, depth)
        return pltpu.make_async_copy(
            source.at[piece, columns_of(h)], own.at[h, p], own_sem
        )

    def load_q(h):
        return pltpu.make_async_copy(q_hbm.at[:, columns_of(h)], q_own.at[h], q_sem)

    def load_ids(i):
        source, target = ((seg_hbm, seg_ref), (mod_hbm, mod_ref))[i]
        return pltpu.make_async_copy(source, target, id_sem.at[i])

    barrier = pltpu.get_barrier_semaphore()
    relay = t == RELAY
    passes = even & has_next & relay
    across = (odd & ~relay & (s + 1 < n)) | passes
    peers = (
        (None, {"tp": 1 - t}),
        (None, {"seq": pair}),
        (has_next, {"seq": s + 2}),
        (has_prev, {"seq": s - 2}),
        (across, {"seq": pair, "tp": 1 - t}),
        (passes, {"seq": s + 2, "tp": 1 - t}),
        (behind & ~relay, {"seq": s - 2, "tp": 1 - t}),
    )
    expected = 0
    for condition, peer in peers:

        def greet(peer=peer):
            pl.semaphore_signal(barrier, inc=1, device_id=peer, device_id_type=MESH)

        if condition is None:
            greet()
            expected = expected + 1
        else:
            pl.when(condition)(greet)
            expected = expected + jnp.where(condition, 1, 0)

    load_ids(0).start()
    for h in range(heads):
        for p in range(PIECES):
            load_piece(h, p).start()
        load_q(h).start()
    load_ids(1).start()
    for i in (0, 1):
        load_ids(i).wait()
    pltpu.make_async_copy(own, own, own_sem).wait()
    pltpu.make_async_copy(q_own, q_own, q_sem).wait()
    pl.semaphore_wait(barrier, expected)

    def remote(source, target, send, recv, where, core=t):
        return pltpu.make_async_remote_copy(
            src_ref=source,
            dst_ref=target,
            send_sem=send,
            recv_sem=recv,
            device_id={"seq": where, "tp": core},
            device_id_type=MESH,
        )

    def flow_a(h, p):
        return remote(own.at[h, p], buf1.at[h, p], send_a, recv_1.at[h, p], pair)

    def flow_b(h, p):
        return remote(own.at[h, p], buf2.at[h, p], send_b, recv_2.at[h, p], s + 2)

    def flow_c(h, p):
        return remote(buf2.at[h, p], buf1.at[h, p], send_c.at[h], recv_1.at[h, p], pair)

    def flow_d(i, p):
        return remote(
            own.at[last - i, p],
            hop.at[t, i, p],
            hop_send.at[t, i, p],
            hop_recv.at[t, i, p],
            pair,
            RELAY,
        )

    def hop_in(i, p, core):
        return remote(
            own.at[last - i, p],
            hop.at[core, i, p],
            hop_send.at[core, i, p],
            hop_recv.at[core, i, p],
            pair,
        )

    def flow_e(i, p, core):
        return remote(
            hop.at[core, i, p],
            buf1.at[last - i, p],
            hop_send.at[core, i, p],
            recv_1.at[last - i, p],
            s + 2,
            core,
        )

    def ask(i):
        return remote(
            q_own.at[kept + i], q_next.at[i], ask_sem.at[0, i], ask_sem.at[1, i], s - 2
        )

    def answer(i):
        return remote(
            part_out.at[i], part_in.at[i], part_sem.at[0, i], part_sem.at[1, i], s + 2
        )

    def answer_lse(i):
        return remote(lse_out.at[i], lse_in.at[i], lse_sem.at[0, i], lse_sem.at[1, i], s + 2)

    def forwards(h):
        return odd & has_prev & (h < beside)

    def seg_a():
        return remote(seg_ref, seg1, seg_send.at[0], seg_recv.at[0], pair)

    def seg_b():
        return remote(seg_ref, seg2, seg_send.at[1], seg_recv.at[1], s + 2)

    def seg_c():
        return remote(seg2, seg1, seg_send.at[2], seg_recv.at[0], pair)

    def seg_d():
        return remote(seg_ref, seg_next, seg_send.at[3], seg_recv.at[2], s - 2)

    @pl.when(even)
    def _():
        seg_a().start()

    @pl.when(has_next)
    def _():
        seg_b().start()

    @pl.when(asks)
    def _():
        seg_d().start()
        for i in range(QUERY):
            ask(i).start()

    for i in range(DIRECT):

        @pl.when(i < leaving)
        def _():
            for p in range(PIECES):
                flow_d(i, p).start()

    def send(h, carry):
        for p in range(PIECES):

            @pl.when(has_next & (odd | (h < kept)))
            def _():
                flow_b(h, p).start()

            @pl.when(even)
            def _():
                flow_a(h, p).start()

        return carry

    lax.fori_loop(0, heads, send, 0)

    def arrive(h, pieces):
        for p in pieces:

            @pl.when(s >= 1)
            def _():
                flow_a(h, p).wait_recv()

    def reach(h, p):
        @pl.when(has_prev)
        def _():
            flow_b(h, p).wait_recv()

        @pl.when(forwards(h))
        def _():
            flow_c(h, p).start()

    def pass_on(h):
        for p in range(PIECES):
            reach(h, p)

    @pl.when(odd & has_prev)
    def _():
        seg_b().wait_recv()
        seg_c().start()
        pass_on(0)

    @pl.when(s < 1)
    def _():
        buf1[...] = jnp.zeros_like(buf1)
        seg1[...] = jnp.full_like(seg1, -1)

    @pl.when(s < 2)
    def _():
        buf2[...] = jnp.zeros_like(buf2)
        seg2[...] = jnp.full_like(seg2, -1)
        part_in[...] = jnp.zeros_like(part_in)
        lse_in[...] = jnp.full_like(lse_in, NEVER)

    def column(row):
        return jnp.transpose(jnp.broadcast_to(row, (HEAD_DIM, rows)))

    query_seg = column(seg_ref[...])[:, :1]
    query_pos = lax.broadcasted_iota(jnp.int32, (rows, rows), 0)
    key_pos = lax.broadcasted_iota(jnp.int32, (rows, rows), 1)
    allowed = (query_seg == seg_ref[...]) & (key_pos <= query_pos)
    bias[:, :rows] = jnp.where(allowed, 0.0, -jnp.inf)
    squares[...] = jnp.zeros_like(squares)
    image_ref[...] = column(mod_ref[...])

    def scores_of(query, key):
        return scale * lax.dot_general(
            query, key, (((1,), (1,)), ((), ())), preferred_element_type=jnp.float32
        )

    def relay_head(i):
        @pl.when(passes & (i < passing))
        def _():
            for core in (0, 1):
                for p in range(PIECES):
                    hop_in(i, p, core).wait_recv()
                    flow_e(i, p, core).start()

    def attend_for(i):
        h = shipped[i]
        ask(i).wait_recv()
        key = own[h, :half].reshape(rows, HEAD_DIM)
        value = own[h, half:].reshape(rows, HEAD_DIM)
        score = scores_of(q_next[i], key) + bias_next[...]
        top = jnp.max(score, axis=1, keepdims=True)
        weight = jnp.exp(score - top)
        total = jnp.sum(weight, axis=1, keepdims=True)
        acc = jnp.dot(weight.astype(jnp.bfloat16), value, preferred_element_type=jnp.float32)
        part_out[i] = (acc * (1.0 / total)).astype(jnp.bfloat16)
        lse = jnp.broadcast_to(top + jnp.log(total), (rows, HEAD_DIM))
        lse_out[i] = jnp.transpose(lse)[:8]

    def send_answer(i):
        answer_lse(i).start()
        answer(i).start()

    @pl.when(answers)
    def _():
        seg_d().wait_recv()
        asker = column(seg_next[...])[:, :1]
        bias_next[...] = jnp.where(asker == seg_ref[...], 0.0, NEVER)
        relayed = 0
        for i in range(QUERY):
            attend_for(i)
            if i > 0:
                send_answer(i - 1)
            while relayed < DIRECT and i + 1 >= 2 * relayed + 1:
                relay_head(relayed)
                relayed += 1
        send_answer(QUERY - 1)
        for i in range(relayed, DIRECT):
            relay_head(i)

    @pl.when(asks)
    def _():
        seg_b().wait_recv()

    @pl.when(s >= 1)
    def _():
        seg_a().wait_recv()

    bias[:, rows : 2 * rows] = jnp.where(query_seg == seg1[...], 0.0, -jnp.inf)
    bias[:, 2 * rows :] = jnp.where(query_seg == seg2[...], 0.0, -jnp.inf)

    def scores_with(h, block, i):
        key = block[h, :half].reshape(rows, HEAD_DIM)
        return scores_of(q_own[h], key) + bias[:, i * rows : (i + 1) * rows]

    def product(weight, value):
        return jnp.dot(weight.astype(jnp.bfloat16), value, preferred_element_type=jnp.float32)

    def values_of(block, h):
        return block[h, half:].reshape(rows, HEAD_DIM)

    def finish(h, acc, total):
        attended = (acc * (1.0 / total)).astype(jnp.bfloat16)
        att[h] = attended
        wide = attended.astype(jnp.float32)
        return wide * wide

    def head(h, pieces_apart):
        @pl.when(even)
        def _():
            for p in range(half):
                reach(h, p)

        near = scores_with(h, own, 0)
        far = scores_with(h, buf2, 2)
        arrive(h, range(half))
        middle = scores_with(h, buf1, 1)
        top = jnp.max(jnp.maximum(jnp.maximum(near, middle), far), axis=1, keepdims=True)
        near = jnp.exp(near - top)
        far = jnp.exp(far - top)
        middle = jnp.exp(middle - top)
        total = jnp.sum(near + middle + far, axis=1, keepdims=True)
        acc = product(near, values_of(own, h))

        @pl.when(even)
        def _():
            for p in range(half, PIECES):
                reach(h, p)

        if pieces_apart:
            acc = acc + product(far, values_of(buf2, h))
            for p in range(half, PIECES):
                arrive(h, (p,))
                part = middle[:, (p - half) * depth : (p - half + 1) * depth]
                acc = acc + product(part, buf1[h, p])
        else:
            arrive(h, range(half, PIECES))
            acc = acc + product(far, values_of(buf2, h)) + product(middle, values_of(buf1, h))
        return finish(h, acc, total)

    def merged(i):
        h = kept + i
        near = scores_with(h, own, 0)

        @pl.when(asks)
        def _():
            answer_lse(i).wait_recv()
            answer(i).wait_recv()

        lse = column(lse_in[i, :1])[:, :1]
        first_top = jnp.maximum(jnp.max(near, axis=1, keepdims=True), lse)
        near = jnp.exp(near - first_top)
        far = jnp.exp(lse - first_top)
        first_total = jnp.sum(near, axis=1, keepdims=True) + far
        acc = product(near, values_of(own, h)) + far * part_in[i].astype(jnp.float32)
        arrive(h, range(half))
        middle = scores_with(h, buf1, 1)
        top = jnp.maximum(jnp.max(middle, axis=1, keepdims=True), first_top)
        middle = jnp.exp(middle - top)
        again = jnp.exp(first_top - top)
        total = jnp.sum(middle, axis=1, keepdims=True) + again * first_total
        acc = acc * again
        arrive(h, range(half, PIECES))
        acc = acc + product(middle, values_of(buf1, h))
        return finish(h, acc, total)

    def one(h, carry):
        @pl.when(odd & (h + 1 < beside))
        def _():
            pass_on(h + 1)

        @pl.when(odd & (h >= beside))
        def _():
            pass_on(h)

        squares[...] += head(h, False)
        return carry

    def conclude(wide):
        partial = jnp.sum(squares[...] + wide, axis=1, keepdims=True)
        mine[...] = jnp.broadcast_to(partial, mine.shape)

    lax.fori_loop(0, jnp.where(odd, last, kept), one, 0)

    @pl.when(odd & has_prev & (beside < heads))
    def _():
        pass_on(last)

    @pl.when(odd)
    def _():
        conclude(head(last, True))

    def shipped_at(j):
        waiting = QUERY - 1 - arriving
        early = jnp.where(j < waiting, j, QUERY - 1 - (j - waiting))
        return jnp.where(j == QUERY - 1, waiting, early)

    def joined(j, carry):
        squares[...] += merged(shipped_at(j))
        return carry

    @pl.when(even)
    def _():
        lax.fori_loop(0, QUERY - 1, joined, 0)
        conclude(merged(shipped_at(QUERY - 1)))

    swap = pltpu.make_async_remote_copy(
        src_ref=mine,
        dst_ref=theirs,
        send_sem=sq_sem.at[0],
        recv_sem=sq_sem.at[1],
        device_id={"tp": 1 - t},
        device_id_type=MESH,
    )
    swap.start()

    def sent(ref, send):
        remote(ref, ref, send, recv_1.at[0, 0], pair).wait_send()

    for i in range(DIRECT):

        @pl.when(i < leaving)
        def _():
            for p in range(PIECES):
                flow_d(i, p).wait_send()

        @pl.when(passes & (i < passing))
        def _():
            for core in (0, 1):
                for p in range(PIECES):
                    flow_e(i, p, core).wait_send()

    @pl.when(asks)
    def _():
        seg_d().wait_send()
        for i in range(QUERY):
            ask(i).wait_send()

    @pl.when(answers)
    def _():
        for i in range(QUERY):
            answer(i).wait_send()
            answer_lse(i).wait_send()

    @pl.when(even)
    def _():
        seg_a().wait_send()
        sent(own, send_a)

    @pl.when(has_next)
    def _():
        seg_b().wait_send()
        sent(own.at[:kept], send_b)

    @pl.when(odd & has_next)
    def _():
        sent(own.at[kept:], send_b)

    @pl.when(odd & has_prev)
    def _():
        seg_c().wait_send()

    for h in range(heads):

        @pl.when(forwards(h))
        def _():
            sent(buf2.at[h], send_c.at[h])

    swap.wait_recv()
    mean_square = (mine[...] + theirs[...]) / (HEADS * HEAD_DIM)
    inverse_ref[...] = lax.rsqrt(mean_square + 1e-05)
    swap.wait_send()


def blend(heads, att, inverse_ref, image_ref, gain_ref, out_hbm, staged, out_sem):
    inverse = inverse_ref[...]
    image = image_ref[...] == 1
    copies = []
    for h in range(heads):
        columns = slice(h * HEAD_DIM, (h + 1) * HEAD_DIM)
        gain = jnp.where(image, gain_ref[1:2, columns], gain_ref[0:1, columns])
        staged[h] = (att[h].astype(jnp.float32) * inverse * gain).astype(staged.dtype)
        copy = pltpu.make_async_copy(
            staged.at[h], out_hbm.at[:, pl.ds(h * HEAD_DIM, HEAD_DIM)], out_sem.at[h]
        )
        copy.start()
        copies.append(copy)
    for copy in copies:
        copy.wait()


def on_device(n, queries, keys, values, segment_ids, modality, norm_gain):
    rows, width = queries.shape
    heads = width // HEAD_DIM
    vmem = pl.BlockSpec(memory_space=pltpu.VMEM)
    hbm = pl.BlockSpec(memory_space=pltpu.HBM)
    depth = 2 * rows // PIECES
    block = pltpu.VMEM((heads, PIECES, depth, HEAD_DIM), jnp.bfloat16)
    asked = pltpu.VMEM((QUERY, rows, HEAD_DIM), jnp.bfloat16)
    ids = pltpu.VMEM((1, rows), jnp.int32)
    flow = pltpu.SemaphoreType.DMA((heads, PIECES))
    att, inverse, image = pl.pallas_call(
        functools.partial(kernel, n, heads, rows),
        out_shape=(
            pltpu.VMEM((heads, rows, HEAD_DIM), jnp.bfloat16),
            pltpu.VMEM((rows, HEAD_DIM), jnp.float32),
            pltpu.VMEM((rows, HEAD_DIM), jnp.int32),
        ),
        in_specs=[hbm, hbm, hbm, hbm, hbm],
        out_specs=(vmem, vmem, vmem),
        scratch_shapes=[
            pltpu.VMEM((heads, rows, HEAD_DIM), jnp.bfloat16),
            block,
            block,
            block,
            pltpu.VMEM((2, DIRECT, PIECES, depth, HEAD_DIM), jnp.bfloat16),
            asked,
            asked,
            pltpu.VMEM((QUERY, 8, rows), jnp.float32),
            asked,
            pltpu.VMEM((QUERY, 8, rows), jnp.float32),
            ids,
            ids,
            ids,
            ids,
            ids,
            pltpu.VMEM((rows, (REACH + 1) * rows), jnp.float32),
            pltpu.VMEM((rows, rows), jnp.float32),
            pltpu.VMEM((rows, HEAD_DIM), jnp.float32),
            pltpu.VMEM((rows, HEAD_DIM), jnp.float32),
            pltpu.VMEM((rows, HEAD_DIM), jnp.float32),
            pltpu.SemaphoreType.DMA,
            pltpu.SemaphoreType.DMA,
            pltpu.SemaphoreType.DMA,
            pltpu.SemaphoreType.DMA,
            pltpu.SemaphoreType.DMA((heads,)),
            flow,
            flow,
            pltpu.SemaphoreType.DMA((2, DIRECT, PIECES)),
            pltpu.SemaphoreType.DMA((2, DIRECT, PIECES)),
            pltpu.SemaphoreType.DMA((2, QUERY)),
            pltpu.SemaphoreType.DMA((2, QUERY)),
            pltpu.SemaphoreType.DMA((2, QUERY)),
            pltpu.SemaphoreType.DMA((2,)),
            pltpu.SemaphoreType.DMA((4,)),
            pltpu.SemaphoreType.DMA((3,)),
            pltpu.SemaphoreType.DMA((2,)),
        ],
        compiler_params=pltpu.CompilerParams(
            collective_id=0, has_side_effects=True
        ),
    )(queries, keys, values, segment_ids.reshape(1, rows), modality.reshape(1, rows))
    return pl.pallas_call(
        functools.partial(blend, heads),
        out_shape=jax.ShapeDtypeStruct((rows, width), jnp.bfloat16),
        in_specs=[vmem, vmem, vmem, vmem],
        out_specs=hbm,
        scratch_shapes=[
            pltpu.VMEM((heads, rows, HEAD_DIM), jnp.bfloat16),
            pltpu.SemaphoreType.DMA((heads,)),
        ],
        compiler_params=pltpu.CompilerParams(vmem_limit_bytes=8 * 2**20),
    )(att, inverse, image, norm_gain)


def solution(mesh):
    return jax.shard_map(
        functools.partial(on_device, mesh.shape["seq"]),
        mesh=mesh,
        in_specs=(
            P(("grp", "seq"), "tp"),
            P(("grp", "seq"), "tp"),
            P(("grp", "seq"), "tp"),
            P(("grp", "seq")),
            P(("grp", "seq")),
            P(None, "tp"),
        ),
        out_specs=P(("grp", "seq"), "tp"),
        check_vma=False,
    )
```

time: 32.7 us -> 30.9 us (0.945)
  Pallas kernels: 32.5 us -> 30.7 us
    pallas_call x1, Pallas kernels: 31.6 us -> 29.8 us  [on_device(): pl.pallas_call(functools.partial(kernel, n, heads, rows), out_shape=(pltp...]
where the time goes in v2:
time: 30.9 us; the launch traced here: 30.7 us
  Pallas kernels  30.7 us (99%)
    pallas_call x1, Pallas kernels, on_device(): pl.pallas_call(functools.partial(kernel, n, heads, rows), out_shape=(pltp...  29.8 us
    pallas_call x1, Pallas kernels, on_device(): pl.pallas_call(functools.partial(blend, heads), out_shape=jax.ShapeDtypeS...  0.88 us

profile of v2, /device:TPU:9, one launch (start us, length us, event | category | flops | bytes accessed | tf_op | source)
XLA Modules:
  0.0 30.7 jit_solution(14823495655453922906)
XLA Ops:
  0.0 0.0 copy-start
  0.0 29.8 %shard_map.64 = (bf16[8,256,128]{2,1,0:T(8,128)(2,1)S(1)}, f32[256,128]{1,0:T(8,128)S(1)}, s32[256,128]{1,0:T(8,128)S(1)}) custom-call(bf16[256,1024]{1,0:T(8,128)(2,1)} %q_hbm.1, bf16[256,1024]{1,0:T(8,128)(2,1)} %k_hbm.1, bf16[256,1024]{1,0:T(8,128)(2,1)} %v_hbm.1, s32[1,256]{1,0:T(1,128)} %bitcast.2, s32[1,256]{1,0:T(1,128)} %bitcast.3), custom_call_target="tpu_custom_call" | custom-call | tf_op jit(solution)/shard_map/pallas_call | solution.py:583
  29.8 0.0 copy-done
  29.8 0.9 %shard_map.65 = bf16[256,1024]{1,0:T(8,128)(2,1)} custom-call(bf16[8,256,128]{2,1,0:T(8,128)(2,1)S(1)} %get-tuple-element.8.att, f32[256,128]{1,0:T(8,128)S(1)} %get-tuple-element.9.inverse_ref, s32[256,128]{1,0:T(8,128)S(1)} %get-tuple-element.10.image_ref, f32[2,1024]{1,0:T(2,128)S(1)} %copy-done), custom_call_target="tpu_custom_call" | custom-call | tf_op jit(solution)/shard_map/pallas_call | solution.py:634
Async XLA Ops:
  0.0 29.8 %copy-start = (f32[2,1024]{1,0:T(2,128)S(1)}, f32[2,1024]{1,0:T(2,128)}, u32[]{:S(2)}) copy-start(f32[2,1024]{1,0:T(2,128)} %gain_ref.1) | copy-start | bytes 24580

commit v3 on v2

--- a/solution.py
+++ b/solution.py
@@ -12,10 +12,9 @@
 REACH = 2
 MESH = pl.DeviceIdType.MESH
 PIECES = 2
-DIRECT = 1
-QUERY = 3
+DIRECT = 2
+FEWEST = 2
 NEVER = -1e30
-RELAY = 1
 
 
 def kernel(
@@ -82,18 +81,20 @@
     half = PIECES // 2
     depth = rows // half
     last = heads - 1
-    kept = heads - QUERY
-    shipped = range(kept, heads)
     cuts = n // 2 - 1
     scale = HEAD_DIM ** (-0.5)
 
     def direct_into(block):
-        return DIRECT + 0 * block
+        return FEWEST + ((cuts - block // 2) * (DIRECT - FEWEST)) // max(cuts - 1, 1)
 
     leaving = jnp.where(ahead, direct_into(s + 1), 0)
     passing = jnp.where(even & has_next, direct_into(s + 2), 0)
     arriving = jnp.where(asks, direct_into(s), 0)
     beside = heads - jnp.where(odd & has_prev, direct_into(s - 1), 0)
+
+    def turn(j, direct):
+        mixed = jnp.where(lax.rem(j, 2) == 0, last - j // 2, j // 2)
+        return jnp.where(j < 2 * direct, mixed, j - direct)
 
     def columns_of(h):
         return pl.ds(h * HEAD_DIM, HEAD_DIM)
@@ -113,17 +114,11 @@
         return pltpu.make_async_copy(source, target, id_sem.at[i])
 
     barrier = pltpu.get_barrier_semaphore()
-    relay = t == RELAY
-    passes = even & has_next & relay
-    across = (odd & ~relay & (s + 1 < n)) | passes
     peers = (
         (None, {"tp": 1 - t}),
         (None, {"seq": pair}),
         (has_next, {"seq": s + 2}),
         (has_prev, {"seq": s - 2}),
-        (across, {"seq": pair, "tp": 1 - t}),
-        (passes, {"seq": s + 2, "tp": 1 - t}),
-        (behind & ~relay, {"seq": s - 2, "tp": 1 - t}),
     )
     expected = 0
     for condition, peer in peers:
@@ -150,13 +145,13 @@
     pltpu.make_async_copy(q_own, q_own, q_sem).wait()
     pl.semaphore_wait(barrier, expected)
 
-    def remote(source, target, send, recv, where, core=t):
+    def remote(source, target, send, recv, where):
         return pltpu.make_async_remote_copy(
             src_ref=source,
             dst_ref=target,
             send_sem=send,
             recv_sem=recv,
-            device_id={"seq": where, "tp": core},
+            device_id={"seq": where},
             device_id_type=MESH,
         )
 
@@ -171,36 +166,17 @@
 
     def flow_d(i, p):
         return remote(
-            own.at[last - i, p],
-            hop.at[t, i, p],
-            hop_send.at[t, i, p],
-            hop_recv.at[t, i, p],
-            pair,
-            RELAY,
-        )
-
-    def hop_in(i, p, core):
+            own.at[last - i, p], hop.at[i, p], hop_send.at[i, p], hop_recv.at[i, p], pair
+        )
+
+    def flow_e(i, p):
         return remote(
-            own.at[last - i, p],
-            hop.at[core, i, p],
-            hop_send.at[core, i, p],
-            hop_recv.at[core, i, p],
-            pair,
-        )
-
-    def flow_e(i, p, core):
-        return remote(
-            hop.at[core, i, p],
-            buf1.at[last - i, p],
-            hop_send.at[core, i, p],
-            recv_1.at[last - i, p],
-            s + 2,
-            core,
+            hop.at[i, p], buf1.at[last - i, p], hop_send.at[i, p], recv_1.at[last - i, p], s + 2
         )
 
     def ask(i):
         return remote(
-            q_own.at[kept + i], q_next.at[i], ask_sem.at[0, i], ask_sem.at[1, i], s - 2
+            q_own.at[i], q_next.at[i], ask_sem.at[0, i], ask_sem.at[1, i], s - 2
         )
 
     def answer(i):
@@ -230,15 +206,19 @@
     def _():
         seg_a().start()
 
-    @pl.when(has_next)
+    @pl.when(odd & has_next)
     def _():
         seg_b().start()
 
     @pl.when(asks)
     def _():
         seg_d().start()
-        for i in range(QUERY):
-            ask(i).start()
+
+        def send_ask(j, carry):
+            ask(turn(j, arriving)).start()
+            return carry
+
+        lax.fori_loop(0, heads, send_ask, 0)
 
     for i in range(DIRECT):
 
@@ -250,7 +230,7 @@
     def send(h, carry):
         for p in range(PIECES):
 
-            @pl.when(has_next & (odd | (h < kept)))
+            @pl.when(odd & has_next)
             def _():
                 flow_b(h, p).start()
 
@@ -270,7 +250,7 @@
                 flow_a(h, p).wait_recv()
 
     def reach(h, p):
-        @pl.when(has_prev)
+        @pl.when(odd & has_prev)
         def _():
             flow_b(h, p).wait_recv()
 
@@ -317,18 +297,14 @@
         )
 
     def relay_head(i):
-        @pl.when(passes & (i < passing))
-        def _():
-            for core in (0, 1):
-                for p in range(PIECES):
-                    hop_in(i, p, core).wait_recv()
-                    flow_e(i, p, core).start()
+        for p in range(PIECES):
+            flow_d(i, p).wait_recv()
+            flow_e(i, p).start()
 
     def attend_for(i):
-        h = shipped[i]
         ask(i).wait_recv()
-        key = own[h, :half].reshape(rows, HEAD_DIM)
-        value = own[h, half:].reshape(rows, HEAD_DIM)
+        key = own[i, :half].reshape(rows, HEAD_DIM)
+        value = own[i, half:].reshape(rows, HEAD_DIM)
         score = scores_of(q_next[i], key) + bias_next[...]
         top = jnp.max(score, axis=1, keepdims=True)
         weight = jnp.exp(score - top)
@@ -347,21 +323,23 @@
         seg_d().wait_recv()
         asker = column(seg_next[...])[:, :1]
         bias_next[...] = jnp.where(asker == seg_ref[...], 0.0, NEVER)
-        relayed = 0
-        for i in range(QUERY):
-            attend_for(i)
-            if i > 0:
-                send_answer(i - 1)
-            while relayed < DIRECT and i + 1 >= 2 * relayed + 1:
-                relay_head(relayed)
-                relayed += 1
-        send_answer(QUERY - 1)
-        for i in range(relayed, DIRECT):
-            relay_head(i)
-
-    @pl.when(asks)
-    def _():
-        seg_b().wait_recv()
+
+        def attend_next(j, carry):
+            h = turn(j, passing)
+            attend_for(h)
+
+            @pl.when(j > 0)
+            def _():
+                send_answer(turn(j - 1, passing))
+
+            @pl.when((lax.rem(j, 2) == 0) & (j < 2 * passing))
+            def _():
+                relay_head(j // 2)
+
+            return carry
+
+        lax.fori_loop(0, heads, attend_next, 0)
+        send_answer(turn(last, passing))
 
     @pl.when(s >= 1)
     def _():
@@ -387,11 +365,6 @@
         return wide * wide
 
     def head(h, pieces_apart):
-        @pl.when(even)
-        def _():
-            for p in range(half):
-                reach(h, p)
-
         near = scores_with(h, own, 0)
         far = scores_with(h, buf2, 2)
         arrive(h, range(half))
@@ -403,11 +376,6 @@
         total = jnp.sum(near + middle + far, axis=1, keepdims=True)
         acc = product(near, values_of(own, h))
 
-        @pl.when(even)
-        def _():
-            for p in range(half, PIECES):
-                reach(h, p)
-
         if pieces_apart:
             acc = acc + product(far, values_of(buf2, h))
             for p in range(half, PIECES):
@@ -419,21 +387,32 @@
             acc = acc + product(far, values_of(buf2, h)) + product(middle, values_of(buf1, h))
         return finish(h, acc, total)
 
-    def merged(i):
-        h = kept + i
+    def merged(h, apart):
         near = scores_with(h, own, 0)
 
         @pl.when(asks)
         def _():
-            answer_lse(i).wait_recv()
-            answer(i).wait_recv()
-
-        lse = column(lse_in[i, :1])[:, :1]
+            answer_lse(h).wait_recv()
+            answer(h).wait_recv()
+
+        lse = column(lse_in[h, :1])[:, :1]
+        if not apart:
+            arrive(h, range(half))
+            middle = scores_with(h, buf1, 1)
+            top = jnp.max(jnp.maximum(near, middle), axis=1, keepdims=True)
+            top = jnp.maximum(top, lse)
+            near = jnp.exp(near - top)
+            middle = jnp.exp(middle - top)
+            far = jnp.exp(lse - top)
+            total = jnp.sum(near + middle, axis=1, keepdims=True) + far
+            acc = product(near, values_of(own, h)) + far * part_in[h].astype(jnp.float32)
+            arrive(h, range(half, PIECES))
+            return finish(h, acc + product(middle, values_of(buf1, h)), total)
         first_top = jnp.maximum(jnp.max(near, axis=1, keepdims=True), lse)
         near = jnp.exp(near - first_top)
         far = jnp.exp(lse - first_top)
         first_total = jnp.sum(near, axis=1, keepdims=True) + far
-        acc = product(near, values_of(own, h)) + far * part_in[i].astype(jnp.float32)
+        acc = product(near, values_of(own, h)) + far * part_in[h].astype(jnp.float32)
         arrive(h, range(half))
         middle = scores_with(h, buf1, 1)
         top = jnp.maximum(jnp.max(middle, axis=1, keepdims=True), first_top)
@@ -442,15 +421,14 @@
         total = jnp.sum(middle, axis=1, keepdims=True) + again * first_total
         acc = acc * again
         arrive(h, range(half, PIECES))
-        acc = acc + product(middle, values_of(buf1, h))
-        return finish(h, acc, total)
+        return finish(h, acc + product(middle, values_of(buf1, h)), total)
 
     def one(h, carry):
-        @pl.when(odd & (h + 1 < beside))
+        @pl.when(h + 1 < beside)
         def _():
             pass_on(h + 1)
 
-        @pl.when(odd & (h >= beside))
+        @pl.when(h >= beside)
         def _():
             pass_on(h)
 
@@ -461,29 +439,24 @@
         partial = jnp.sum(squares[...] + wide, axis=1, keepdims=True)
         mine[...] = jnp.broadcast_to(partial, mine.shape)
 
-    lax.fori_loop(0, jnp.where(odd, last, kept), one, 0)
-
-    @pl.when(odd & has_prev & (beside < heads))
-    def _():
-        pass_on(last)
-
     @pl.when(odd)
     def _():
+        lax.fori_loop(0, last, one, 0)
+
+        @pl.when(beside < heads)
+        def _():
+            pass_on(last)
+
         conclude(head(last, True))
 
-    def shipped_at(j):
-        waiting = QUERY - 1 - arriving
-        early = jnp.where(j < waiting, j, QUERY - 1 - (j - waiting))
-        return jnp.where(j == QUERY - 1, waiting, early)
-
     def joined(j, carry):
-        squares[...] += merged(shipped_at(j))
+        squares[...] += merged(turn(j, arriving), False)
         return carry
 
     @pl.when(even)
     def _():
-        lax.fori_loop(0, QUERY - 1, joined, 0)
-        conclude(merged(shipped_at(QUERY - 1)))
+        lax.fori_loop(0, last, joined, 0)
+        conclude(merged(turn(last, arriving), True))
 
     swap = pltpu.make_async_remote_copy(
         src_ref=mine,
@@ -505,21 +478,20 @@
             for p in range(PIECES):
                 flow_d(i, p).wait_send()
 
-        @pl.when(passes & (i < passing))
-        def _():
-            for core in (0, 1):
-                for p in range(PIECES):
-                    flow_e(i, p, core).wait_send()
+        @pl.when(i < passing)
+        def _():
+            for p in range(PIECES):
+                flow_e(i, p).wait_send()
 
     @pl.when(asks)
     def _():
         seg_d().wait_send()
-        for i in range(QUERY):
+        for i in range(heads):
             ask(i).wait_send()
 
     @pl.when(answers)
     def _():
-        for i in range(QUERY):
+        for i in range(heads):
             answer(i).wait_send()
             answer_lse(i).wait_send()
 
@@ -528,14 +500,10 @@
         seg_a().wait_send()
         sent(own, send_a)
 
-    @pl.when(has_next)
+    @pl.when(odd & has_next)
     def _():
         seg_b().wait_send()
-        sent(own.at[:kept], send_b)
-
-    @pl.when(odd & has_next)
-    def _():
-        sent(own.at[kept:], send_b)
+        sent(own, send_b)
 
     @pl.when(odd & has_prev)
     def _():
@@ -577,7 +545,7 @@
     hbm = pl.BlockSpec(memory_space=pltpu.HBM)
     depth = 2 * rows // PIECES
     block = pltpu.VMEM((heads, PIECES, depth, HEAD_DIM), jnp.bfloat16)
-    asked = pltpu.VMEM((QUERY, rows, HEAD_DIM), jnp.bfloat16)
+    asked = pltpu.VMEM((heads, rows, HEAD_DIM), jnp.bfloat16)
     ids = pltpu.VMEM((1, rows), jnp.int32)
     flow = pltpu.SemaphoreType.DMA((heads, PIECES))
     att, inverse, image = pl.pallas_call(
@@ -594,12 +562,12 @@
             block,
             block,
             block,
-            pltpu.VMEM((2, DIRECT, PIECES, depth, HEAD_DIM), jnp.bfloat16),
+            pltpu.VMEM((DIRECT, PIECES, depth, HEAD_DIM), jnp.bfloat16),
             asked,
             asked,
-            pltpu.VMEM((QUERY, 8, rows), jnp.float32),
+            pltpu.VMEM((heads, 8, rows), jnp.float32),
             asked,
-            pltpu.VMEM((QUERY, 8, rows), jnp.float32),
+            pltpu.VMEM((heads, 8, rows), jnp.float32),
             ids,
             ids,
             ids,
@@ -617,11 +585,11 @@
             pltpu.SemaphoreType.DMA((heads,)),
             flow,
             flow,
-            pltpu.SemaphoreType.DMA((2, DIRECT, PIECES)),
-            pltpu.SemaphoreType.DMA((2, DIRECT, PIECES)),
-            pltpu.SemaphoreType.DMA((2, QUERY)),
-            pltpu.SemaphoreType.DMA((2, QUERY)),
-            pltpu.SemaphoreType.DMA((2, QUERY)),
+            pltpu.SemaphoreType.DMA((DIRECT, PIECES)),
+            pltpu.SemaphoreType.DMA((DIRECT, PIECES)),
+            pltpu.SemaphoreType.DMA((2, heads)),
+            pltpu.SemaphoreType.DMA((2, heads)),
+            pltpu.SemaphoreType.DMA((2, heads)),
             pltpu.SemaphoreType.DMA((2,)),
             pltpu.SemaphoreType.DMA((4,)),
             pltpu.SemaphoreType.DMA((3,)),

time: 30.9 us -> 30 us (0.971)
  Pallas kernels: 30.7 us -> 29.8 us
    pallas_call x1, Pallas kernels: 29.8 us -> 28.9 us  [on_device(): pl.pallas_call(functools.partial(kernel, n, heads, rows), out_shape=(pltp...]
where the time goes in v3:
time: 30 us; the launch traced here: 29.8 us
  Pallas kernels  29.8 us (99%)
    pallas_call x1, Pallas kernels, on_device(): pl.pallas_call(functools.partial(kernel, n, heads, rows), out_shape=(pltp...  28.9 us
    pallas_call x1, Pallas kernels, on_device(): pl.pallas_call(functools.partial(blend, heads), out_shape=jax.ShapeDtypeS...  0.88 us

profile of v3, /device:TPU:9, one launch (start us, length us, event | category | flops | bytes accessed | tf_op | source)
XLA Modules:
  0.0 29.8 jit_solution(6833217370068200086)
XLA Ops:
  0.0 0.0 copy-start
  0.0 28.9 %shard_map.64 = (bf16[8,256,128]{2,1,0:T(8,128)(2,1)S(1)}, f32[256,128]{1,0:T(8,128)S(1)}, s32[256,128]{1,0:T(8,128)S(1)}) custom-call(bf16[256,1024]{1,0:T(8,128)(2,1)} %q_hbm.1, bf16[256,1024]{1,0:T(8,128)(2,1)} %k_hbm.1, bf16[256,1024]{1,0:T(8,128)(2,1)} %v_hbm.1, s32[1,256]{1,0:T(1,128)} %bitcast.2, s32[1,256]{1,0:T(1,128)} %bitcast.3), custom_call_target="tpu_custom_call" | custom-call | tf_op jit(solution)/shard_map/pallas_call | solution.py:551
  29.0 0.0 copy-done
  29.0 0.9 %shard_map.65 = bf16[256,1024]{1,0:T(8,128)(2,1)} custom-call(bf16[8,256,128]{2,1,0:T(8,128)(2,1)S(1)} %get-tuple-element.8.att, f32[256,128]{1,0:T(8,128)S(1)} %get-tuple-element.9.inverse_ref, s32[256,128]{1,0:T(8,128)S(1)} %get-tuple-element.10.image_ref, f32[2,1024]{1,0:T(2,128)S(1)} %copy-done), custom_call_target="tpu_custom_call" | custom-call | tf_op jit(solution)/shard_map/pallas_call | solution.py:602
Async XLA Ops:
  0.0 29.0 %copy-start = (f32[2,1024]{1,0:T(2,128)S(1)}, f32[2,1024]{1,0:T(2,128)}, u32[]{:S(2)}) copy-start(f32[2,1024]{1,0:T(2,128)} %gain_ref.1) | copy-start | bytes 24580

commit v4 on v3

--- a/solution.py
+++ b/solution.py
@@ -12,9 +12,11 @@
 REACH = 2
 MESH = pl.DeviceIdType.MESH
 PIECES = 2
-DIRECT = 2
-FEWEST = 2
+MOST = (4, 6)
+LEAST = (4, 2)
 NEVER = -1e30
+KEPT = 2
+SHIPPER = 0
 
 
 def kernel(
@@ -44,6 +46,7 @@
     seg1,
     seg2,
     seg_next,
+    seg_beside,
     bias,
     bias_next,
     squares,
@@ -77,24 +80,35 @@
     asks = even & has_prev
     answers = even & has_next
     pair = s + 1 - 2 * lax.rem(s, 2)
+    ships = odd & (t == SHIPPER)
+    serves = even & (t == SHIPPER)
+    keeps = t != SHIPPER
 
     half = PIECES // 2
     depth = rows // half
     last = heads - 1
+    turns = heads - KEPT
     cuts = n // 2 - 1
     scale = HEAD_DIM ** (-0.5)
 
     def direct_into(block):
-        return FEWEST + ((cuts - block // 2) * (DIRECT - FEWEST)) // max(cuts - 1, 1)
-
+        top = jnp.where(t == 0, MOST[0], MOST[1])
+        low = jnp.where(t == 0, LEAST[0], LEAST[1])
+        return low + ((cuts - block // 2) * (top - low)) // max(cuts - 1, 1)
+
+    deepest = (max(MOST + LEAST) + PIECES - 1) // PIECES
     leaving = jnp.where(ahead, direct_into(s + 1), 0)
     passing = jnp.where(even & has_next, direct_into(s + 2), 0)
     arriving = jnp.where(asks, direct_into(s), 0)
-    beside = heads - jnp.where(odd & has_prev, direct_into(s - 1), 0)
+    skipped = jnp.where(odd & has_prev, direct_into(s - 1), 0)
+    beside = heads - skipped // PIECES
+
+    def unit(i, p):
+        return PIECES * i + PIECES - 1 - p
 
     def turn(j, direct):
-        mixed = jnp.where(lax.rem(j, 2) == 0, last - j // 2, j // 2)
-        return jnp.where(j < 2 * direct, mixed, j - direct)
+        mixed = jnp.where(lax.rem(j, 2) == 0, last - j // 2, KEPT + j // 2)
+        return jnp.where(j < 2 * (direct // PIECES), mixed, KEPT + j - direct // PIECES)
 
     def columns_of(h):
         return pl.ds(h * HEAD_DIM, HEAD_DIM)
@@ -162,7 +176,7 @@
         return remote(own.at[h, p], buf2.at[h, p], send_b, recv_2.at[h, p], s + 2)
 
     def flow_c(h, p):
-        return remote(buf2.at[h, p], buf1.at[h, p], send_c.at[h], recv_1.at[h, p], pair)
+        return remote(buf2.at[h, p], buf1.at[h, p], send_c.at[h, p], recv_1.at[h, p], pair)
 
     def flow_d(i, p):
         return remote(
@@ -184,11 +198,20 @@
             part_out.at[i], part_in.at[i], part_sem.at[0, i], part_sem.at[1, i], s + 2
         )
 
+    def ask_beside():
+        return remote(q_own.at[last], q_next.at[0], ask_sem.at[0, 0], ask_sem.at[1, 0], pair)
+
+    def answer_beside():
+        return remote(part_out.at[0], part_in.at[0], part_sem.at[0, 0], part_sem.at[1, 0], pair)
+
+    def answer_beside_lse():
+        return remote(lse_out.at[0], lse_in.at[0], lse_sem.at[0, 0], lse_sem.at[1, 0], pair)
+
     def answer_lse(i):
         return remote(lse_out.at[i], lse_in.at[i], lse_sem.at[0, i], lse_sem.at[1, i], s + 2)
 
-    def forwards(h):
-        return odd & has_prev & (h < beside)
+    def forwards(h, p):
+        return odd & has_prev & (unit(last - h, p) >= skipped)
 
     def seg_a():
         return remote(seg_ref, seg1, seg_send.at[0], seg_recv.at[0], pair)
@@ -199,6 +222,9 @@
     def seg_c():
         return remote(seg2, seg1, seg_send.at[2], seg_recv.at[0], pair)
 
+    def seg_e():
+        return remote(seg_ref, seg_beside, seg_send.at[4], seg_recv.at[3], pair)
+
     def seg_d():
         return remote(seg_ref, seg_next, seg_send.at[3], seg_recv.at[2], s - 2)
 
@@ -206,7 +232,7 @@
     def _():
         seg_a().start()
 
-    @pl.when(odd & has_next)
+    @pl.when(has_next)
     def _():
         seg_b().start()
 
@@ -218,23 +244,33 @@
             ask(turn(j, arriving)).start()
             return carry
 
-        lax.fori_loop(0, heads, send_ask, 0)
-
-    for i in range(DIRECT):
-
-        @pl.when(i < leaving)
-        def _():
-            for p in range(PIECES):
+        lax.fori_loop(0, turns, send_ask, 0)
+
+    @pl.when(ships)
+    def _():
+        seg_e().start()
+        ask_beside().start()
+
+    @pl.when(ships & has_prev)
+    def _():
+        seg_d().start()
+        ask(last).start()
+
+    for i in range(deepest):
+        for p in reversed(range(PIECES)):
+
+            @pl.when(unit(i, p) < leaving)
+            def _():
                 flow_d(i, p).start()
 
     def send(h, carry):
         for p in range(PIECES):
 
-            @pl.when(odd & has_next)
+            @pl.when(has_next & ((odd & ((h < last) | keeps)) | (h < KEPT)))
             def _():
                 flow_b(h, p).start()
 
-            @pl.when(even)
+            @pl.when(even & ((h < last) | keeps))
             def _():
                 flow_a(h, p).start()
 
@@ -250,11 +286,11 @@
                 flow_a(h, p).wait_recv()
 
     def reach(h, p):
-        @pl.when(odd & has_prev)
+        @pl.when(has_prev)
         def _():
             flow_b(h, p).wait_recv()
 
-        @pl.when(forwards(h))
+        @pl.when(forwards(h, p))
         def _():
             flow_c(h, p).start()
 
@@ -277,8 +313,16 @@
     def _():
         buf2[...] = jnp.zeros_like(buf2)
         seg2[...] = jnp.full_like(seg2, -1)
+
+    @pl.when(s == 0)
+    def _():
         part_in[...] = jnp.zeros_like(part_in)
         lse_in[...] = jnp.full_like(lse_in, NEVER)
+
+    @pl.when(s == 1)
+    def _():
+        part_in[last] = jnp.zeros((rows, HEAD_DIM), part_in.dtype)
+        lse_in[last] = jnp.full((8, rows), NEVER, jnp.float32)
 
     def column(row):
         return jnp.transpose(jnp.broadcast_to(row, (HEAD_DIM, rows)))
@@ -297,14 +341,16 @@
         )
 
     def relay_head(i):
-        for p in range(PIECES):
-            flow_d(i, p).wait_recv()
-            flow_e(i, p).start()
-
-    def attend_for(i):
-        ask(i).wait_recv()
-        key = own[i, :half].reshape(rows, HEAD_DIM)
-        value = own[i, half:].reshape(rows, HEAD_DIM)
+        for p in reversed(range(PIECES)):
+
+            @pl.when(unit(i, p) < passing)
+            def _():
+                flow_d(i, p).wait_recv()
+                flow_e(i, p).start()
+
+    def attend_for(i, h):
+        key = own[h, :half].reshape(rows, HEAD_DIM)
+        value = own[h, half:].reshape(rows, HEAD_DIM)
         score = scores_of(q_next[i], key) + bias_next[...]
         top = jnp.max(score, axis=1, keepdims=True)
         weight = jnp.exp(score - top)
@@ -314,32 +360,59 @@
         lse = jnp.broadcast_to(top + jnp.log(total), (rows, HEAD_DIM))
         lse_out[i] = jnp.transpose(lse)[:8]
 
+    def mask_for(ids):
+        asker = column(ids[...])[:, :1]
+        bias_next[...] = jnp.where(asker == seg_ref[...], 0.0, NEVER)
+
     def send_answer(i):
         answer_lse(i).start()
         answer(i).start()
 
+    @pl.when(serves)
+    def _():
+        seg_e().wait_recv()
+        mask_for(seg_beside)
+        ask_beside().wait_recv()
+        attend_for(0, last)
+
+    @pl.when(has_next & (even | ships))
+    def _():
+        seg_d().wait_recv()
+        mask_for(seg_next)
+
+    @pl.when(serves)
+    def _():
+        answer_beside_lse().start()
+        answer_beside().start()
+
+    @pl.when(ships & has_next)
+    def _():
+        ask(last).wait_recv()
+        attend_for(last, last)
+
     @pl.when(answers)
     def _():
-        seg_d().wait_recv()
-        asker = column(seg_next[...])[:, :1]
-        bias_next[...] = jnp.where(asker == seg_ref[...], 0.0, NEVER)
-
         def attend_next(j, carry):
             h = turn(j, passing)
-            attend_for(h)
+            ask(h).wait_recv()
+            attend_for(h, h)
 
             @pl.when(j > 0)
             def _():
                 send_answer(turn(j - 1, passing))
 
-            @pl.when((lax.rem(j, 2) == 0) & (j < 2 * passing))
+            @pl.when((lax.rem(j, 2) == 0) & (j // 2 * PIECES < passing))
             def _():
                 relay_head(j // 2)
 
             return carry
 
-        lax.fori_loop(0, heads, attend_next, 0)
-        send_answer(turn(last, passing))
+        lax.fori_loop(0, turns, attend_next, 0)
+        send_answer(turn(turns - 1, passing))
+
+    @pl.when(asks)
+    def _():
+        seg_b().wait_recv()
 
     @pl.when(s >= 1)
     def _():
@@ -364,7 +437,11 @@
         wide = attended.astype(jnp.float32)
         return wide * wide
 
-    def head(h, pieces_apart):
+    @pl.when(ships & has_next)
+    def _():
+        send_answer(last)
+
+    def head(h):
         near = scores_with(h, own, 0)
         far = scores_with(h, buf2, 2)
         arrive(h, range(half))
@@ -376,16 +453,34 @@
         total = jnp.sum(near + middle + far, axis=1, keepdims=True)
         acc = product(near, values_of(own, h))
 
-        if pieces_apart:
-            acc = acc + product(far, values_of(buf2, h))
-            for p in range(half, PIECES):
-                arrive(h, (p,))
-                part = middle[:, (p - half) * depth : (p - half + 1) * depth]
-                acc = acc + product(part, buf1[h, p])
-        else:
-            arrive(h, range(half, PIECES))
-            acc = acc + product(far, values_of(buf2, h)) + product(middle, values_of(buf1, h))
+        arrive(h, range(half, PIECES))
+        acc = acc + product(far, values_of(buf2, h)) + product(middle, values_of(buf1, h))
         return finish(h, acc, total)
+
+    def joined_last():
+        near = scores_with(last, own, 0)
+        top = jnp.max(near, axis=1, keepdims=True)
+        near = jnp.exp(near - top)
+        total = jnp.sum(near, axis=1, keepdims=True)
+        acc = product(near, values_of(own, last))
+
+        @pl.when(has_prev)
+        def _():
+            answer_lse(last).wait_recv()
+            answer(last).wait_recv()
+
+        answer_beside_lse().wait_recv()
+        answer_beside().wait_recv()
+        far_top = column(lse_in[last, :1])[:, :1]
+        middle_top = column(lse_in[0, :1])[:, :1]
+        most = jnp.maximum(top, jnp.maximum(far_top, middle_top))
+        again = jnp.exp(top - most)
+        far = jnp.exp(far_top - most)
+        middle = jnp.exp(middle_top - most)
+        total = again * total + far + middle
+        acc = again * acc + far * part_in[last].astype(jnp.float32)
+        acc = acc + middle * part_in[0].astype(jnp.float32)
+        return finish(last, acc, total)
 
     def merged(h, apart):
         near = scores_with(h, own, 0)
@@ -432,7 +527,7 @@
         def _():
             pass_on(h)
 
-        squares[...] += head(h, False)
+        squares[...] += head(h)
         return carry
 
     def conclude(wide):
@@ -443,11 +538,14 @@
     def _():
         lax.fori_loop(0, last, one, 0)
 
-        @pl.when(beside < heads)
+        @pl.when(ships)
+        def _():
+            conclude(joined_last())
+
+        @pl.when(keeps)
         def _():
             pass_on(last)
-
-        conclude(head(last, True))
+            conclude(head(last))
 
     def joined(j, carry):
         squares[...] += merged(turn(j, arriving), False)
@@ -455,8 +553,14 @@
 
     @pl.when(even)
     def _():
-        lax.fori_loop(0, last, joined, 0)
-        conclude(merged(turn(last, arriving), True))
+        def kept(h, carry):
+            pass_on(h)
+            squares[...] += head(h)
+            return carry
+
+        lax.fori_loop(0, KEPT, kept, 0)
+        lax.fori_loop(0, turns - 1, joined, 0)
+        conclude(merged(turn(turns - 1, arriving), True))
 
     swap = pltpu.make_async_remote_copy(
         src_ref=mine,
@@ -471,49 +575,81 @@
     def sent(ref, send):
         remote(ref, ref, send, recv_1.at[0, 0], pair).wait_send()
 
-    for i in range(DIRECT):
-
-        @pl.when(i < leaving)
-        def _():
-            for p in range(PIECES):
+    for i in range(deepest):
+        for p in range(PIECES):
+
+            @pl.when(unit(i, p) < leaving)
+            def _():
                 flow_d(i, p).wait_send()
 
-        @pl.when(i < passing)
-        def _():
-            for p in range(PIECES):
+            @pl.when(unit(i, p) < passing)
+            def _():
                 flow_e(i, p).wait_send()
 
     @pl.when(asks)
     def _():
         seg_d().wait_send()
-        for i in range(heads):
+        for i in range(KEPT, heads):
             ask(i).wait_send()
 
+    @pl.when(ships)
+    def _():
+        seg_e().wait_send()
+        ask_beside().wait_send()
+
+    @pl.when(ships & has_prev)
+    def _():
+        seg_d().wait_send()
+        ask(last).wait_send()
+
+    @pl.when(ships & has_next)
+    def _():
+        answer(last).wait_send()
+        answer_lse(last).wait_send()
+
     @pl.when(answers)
     def _():
-        for i in range(heads):
+        for i in range(KEPT, heads):
             answer(i).wait_send()
             answer_lse(i).wait_send()
 
     @pl.when(even)
     def _():
         seg_a().wait_send()
-        sent(own, send_a)
+        sent(own.at[:last], send_a)
+
+    @pl.when(even & keeps)
+    def _():
+        sent(own.at[last], send_a)
+
+    @pl.when(serves)
+    def _():
+        answer_beside().wait_send()
+        answer_beside_lse().wait_send()
+
+    @pl.when(has_next)
+    def _():
+        seg_b().wait_send()
+        sent(own.at[:KEPT], send_b)
 
     @pl.when(odd & has_next)
     def _():
-        seg_b().wait_send()
-        sent(own, send_b)
+        sent(own.at[KEPT:last], send_b)
+
+    @pl.when(odd & has_next & keeps)
+    def _():
+        sent(own.at[last], send_b)
 
     @pl.when(odd & has_prev)
     def _():
         seg_c().wait_send()
 
     for h in range(heads):
-
-        @pl.when(forwards(h))
-        def _():
-            sent(buf2.at[h], send_c.at[h])
+        for p in range(PIECES):
+
+            @pl.when(forwards(h, p))
+            def _():
+                flow_c(h, p).wait_send()
 
     swap.wait_recv()
     mean_square = (mine[...] + theirs[...]) / (HEADS * HEAD_DIM)
@@ -545,6 +681,7 @@
     hbm = pl.BlockSpec(memory_space=pltpu.HBM)
     depth = 2 * rows // PIECES
     block = pltpu.VMEM((heads, PIECES, depth, HEAD_DIM), jnp.bfloat16)
+    deepest = (max(MOST + LEAST) + PIECES - 1) // PIECES
     asked = pltpu.VMEM((heads, rows, HEAD_DIM), jnp.bfloat16)
     ids = pltpu.VMEM((1, rows), jnp.int32)
     flow = pltpu.SemaphoreType.DMA((heads, PIECES))
@@ -562,12 +699,13 @@
             block,
             block,
             block,
-            pltpu.VMEM((DIRECT, PIECES, depth, HEAD_DIM), jnp.bfloat16),
+            pltpu.VMEM((deepest, PIECES, depth, HEAD_DIM), jnp.bfloat16),
             asked,
             asked,
             pltpu.VMEM((heads, 8, rows), jnp.float32),
             asked,
             pltpu.VMEM((heads, 8, rows), jnp.float32),
+            ids,
             ids,
             ids,
             ids,
@@ -582,17 +720,17 @@
             pltpu.SemaphoreType.DMA,
             pltpu.SemaphoreType.DMA,
             pltpu.SemaphoreType.DMA,
-            pltpu.SemaphoreType.DMA((heads,)),
             flow,
             flow,
-            pltpu.SemaphoreType.DMA((DIRECT, PIECES)),
-            pltpu.SemaphoreType.DMA((DIRECT, PIECES)),
+            flow,
+            pltpu.SemaphoreType.DMA((deepest, PIECES)),
+            pltpu.SemaphoreType.DMA((deepest, PIECES)),
             pltpu.SemaphoreType.DMA((2, heads)),
             pltpu.SemaphoreType.DMA((2, heads)),
             pltpu.SemaphoreType.DMA((2, heads)),
             pltpu.SemaphoreType.DMA((2,)),
+            pltpu.SemaphoreType.DMA((5,)),
             pltpu.SemaphoreType.DMA((4,)),
-            pltpu.SemaphoreType.DMA((3,)),
             pltpu.SemaphoreType.DMA((2,)),
         ],
         compiler_params=pltpu.CompilerParams(

time: 30 us -> 29.5 us (0.983)
  Pallas kernels: 29.8 us -> 29.2 us
    pallas_call x1, Pallas kernels: 28.9 us -> 28.4 us  [on_device(): pl.pallas_call(functools.partial(kernel, n, heads, rows), out_shape=(pltp...]
where the time goes in v4:
time: 29.5 us; the launch traced here: 29.3 us
  Pallas kernels  29.2 us (99%)
    pallas_call x1, Pallas kernels, on_device(): pl.pallas_call(functools.partial(kernel, n, heads, rows), out_shape=(pltp...  28.4 us
    pallas_call x1, Pallas kernels, on_device(): pl.pallas_call(functools.partial(blend, heads), out_shape=jax.ShapeDtypeS...  0.88 us

profile of v4, /device:TPU:9, one launch (start us, length us, event | category | flops | bytes accessed | tf_op | source)
XLA Modules:
  0.0 29.3 jit_solution(14062085303803493232)
XLA Ops:
  0.0 0.0 copy-start
  0.0 28.4 %shard_map.64 = (bf16[8,256,128]{2,1,0:T(8,128)(2,1)S(1)}, f32[256,128]{1,0:T(8,128)S(1)}, s32[256,128]{1,0:T(8,128)S(1)}) custom-call(bf16[256,1024]{1,0:T(8,128)(2,1)} %q_hbm.1, bf16[256,1024]{1,0:T(8,128)(2,1)} %k_hbm.1, bf16[256,1024]{1,0:T(8,128)(2,1)} %v_hbm.1, s32[1,256]{1,0:T(1,128)} %bitcast.2, s32[1,256]{1,0:T(1,128)} %bitcast.3), custom_call_target="tpu_custom_call" | custom-call | tf_op jit(solution)/shard_map/pallas_call | solution.py:688
  28.4 0.0 copy-done
  28.4 0.9 %shard_map.65 = bf16[256,1024]{1,0:T(8,128)(2,1)} custom-call(bf16[8,256,128]{2,1,0:T(8,128)(2,1)S(1)} %get-tuple-element.8.att, f32[256,128]{1,0:T(8,128)S(1)} %get-tuple-element.9.inverse_ref, s32[256,128]{1,0:T(8,128)S(1)} %get-tuple-element.10.image_ref, f32[2,1024]{1,0:T(2,128)S(1)} %copy-done), custom_call_target="tpu_custom_call" | custom-call | tf_op jit(solution)/shard_map/pallas_call | solution.py:740
Async XLA Ops:
  0.0 28.4 %copy-start = (f32[2,1024]{1,0:T(2,128)S(1)}, f32[2,1024]{1,0:T(2,128)}, u32[]{:S(2)}) copy-start(f32[2,1024]{1,0:T(2,128)} %gain_ref.1) | copy-start | bytes 24580

commit v5 on v4

--- a/solution.py
+++ b/solution.py
@@ -15,6 +15,7 @@
 MOST = (4, 6)
 LEAST = (4, 2)
 NEVER = -1e30
+FOLD = 4
 KEPT = 2
 SHIPPER = 0
 
@@ -84,6 +85,7 @@
     serves = even & (t == SHIPPER)
     keeps = t != SHIPPER
 
+    deep = rows // FOLD
     half = PIECES // 2
     depth = rows // half
     last = heads - 1
@@ -380,11 +382,6 @@
         seg_d().wait_recv()
         mask_for(seg_next)
 
-    @pl.when(serves)
-    def _():
-        answer_beside_lse().start()
-        answer_beside().start()
-
     @pl.when(ships & has_next)
     def _():
         ask(last).wait_recv()
@@ -440,6 +437,11 @@
     @pl.when(ships & has_next)
     def _():
         send_answer(last)
+
+    @pl.when(serves)
+    def _():
+        answer_beside_lse().start()
+        answer_beside().start()
 
     def head(h):
         near = scores_with(h, own, 0)
@@ -532,7 +534,11 @@
 
     def conclude(wide):
         partial = jnp.sum(squares[...] + wide, axis=1, keepdims=True)
-        mine[...] = jnp.broadcast_to(partial, mine.shape)
+        strip = lax.broadcasted_iota(jnp.int32, mine.shape, 1) // (HEAD_DIM // FOLD)
+        folded = jnp.broadcast_to(partial[:deep], mine.shape)
+        for g in range(1, FOLD):
+            folded = jnp.where(strip == g, partial[g * deep : (g + 1) * deep], folded)
+        mine[...] = folded
 
     @pl.when(odd)
     def _():
@@ -544,7 +550,10 @@
 
         @pl.when(keeps)
         def _():
-            pass_on(last)
+            @pl.when(beside < heads)
+            def _():
+                pass_on(last)
+
             conclude(head(last))
 
     def joined(j, carry):
@@ -653,7 +662,12 @@
 
     swap.wait_recv()
     mean_square = (mine[...] + theirs[...]) / (HEADS * HEAD_DIM)
-    inverse_ref[...] = lax.rsqrt(mean_square + 1e-05)
+    inverse = lax.rsqrt(mean_square + 1e-05)
+    for g in range(FOLD):
+        lane = g * (HEAD_DIM // FOLD)
+        inverse_ref[g * deep : (g + 1) * deep] = jnp.broadcast_to(
+            inverse[:, lane : lane + 1], (deep, HEAD_DIM)
+        )
     swap.wait_send()
 
 
@@ -714,8 +728,8 @@
             pltpu.VMEM((rows, (REACH + 1) * rows), jnp.float32),
             pltpu.VMEM((rows, rows), jnp.float32),
             pltpu.VMEM((rows, HEAD_DIM), jnp.float32),
-            pltpu.VMEM((rows, HEAD_DIM), jnp.float32),
-            pltpu.VMEM((rows, HEAD_DIM), jnp.float32),
+            pltpu.VMEM((rows // FOLD, HEAD_DIM), jnp.float32),
+            pltpu.VMEM((rows // FOLD, HEAD_DIM), jnp.float32),
             pltpu.SemaphoreType.DMA,
             pltpu.SemaphoreType.DMA,
             pltpu.SemaphoreType.DMA,

time: 29.5 us -> 29.4 us (level)
  no operation moved by 1% of the time
where the time goes in v5:
time: 29.4 us; the launch traced here: 29.2 us
  Pallas kernels  29.2 us (99%)
    pallas_call x1, Pallas kernels, on_device(): pl.pallas_call(functools.partial(kernel, n, heads, rows), out_shape=(pltp...  28.3 us
    pallas_call x1, Pallas kernels, on_device(): pl.pallas_call(functools.partial(blend, heads), out_shape=jax.ShapeDtypeS...  0.88 us

profile of v5, /device:TPU:9, one launch (start us, length us, event | category | flops | bytes accessed | tf_op | source)
XLA Modules:
  0.0 29.2 jit_solution(9312013515148647544)
XLA Ops:
  0.0 0.0 copy-start
  0.0 28.3 %shard_map.64 = (bf16[8,256,128]{2,1,0:T(8,128)(2,1)S(1)}, f32[256,128]{1,0:T(8,128)S(1)}, s32[256,128]{1,0:T(8,128)S(1)}) custom-call(bf16[256,1024]{1,0:T(8,128)(2,1)} %q_hbm.1, bf16[256,1024]{1,0:T(8,128)(2,1)} %k_hbm.1, bf16[256,1024]{1,0:T(8,128)(2,1)} %v_hbm.1, s32[1,256]{1,0:T(1,128)} %bitcast.2, s32[1,256]{1,0:T(1,128)} %bitcast.3), custom_call_target="tpu_custom_call" | custom-call | tf_op jit(solution)/shard_map/pallas_call | solution.py:702
  28.3 0.0 copy-done
  28.3 0.9 %shard_map.65 = bf16[256,1024]{1,0:T(8,128)(2,1)} custom-call(bf16[8,256,128]{2,1,0:T(8,128)(2,1)S(1)} %get-tuple-element.8.att, f32[256,128]{1,0:T(8,128)S(1)} %get-tuple-element.9.inverse_ref, s32[256,128]{1,0:T(8,128)S(1)} %get-tuple-element.10.image_ref, f32[2,1024]{1,0:T(2,128)S(1)} %copy-done), custom_call_target="tpu_custom_call" | custom-call | tf_op jit(solution)/shard_map/pallas_call | solution.py:754
Async XLA Ops:
  0.0 28.3 %copy-start = (f32[2,1024]{1,0:T(2,128)S(1)}, f32[2,1024]{1,0:T(2,128)}, u32[]{:S(2)}) copy-start(f32[2,1024]{1,0:T(2,128)} %gain_ref.1) | copy-start | bytes 24580

commit v6 on v5

--- a/solution.py
+++ b/solution.py
@@ -324,7 +324,7 @@
     @pl.when(s == 1)
     def _():
         part_in[last] = jnp.zeros((rows, HEAD_DIM), part_in.dtype)
-        lse_in[last] = jnp.full((8, rows), NEVER, jnp.float32)
+        lse_in[last] = jnp.full((1, rows), NEVER, jnp.float32)
 
     def column(row):
         return jnp.transpose(jnp.broadcast_to(row, (HEAD_DIM, rows)))
@@ -360,7 +360,7 @@
         acc = jnp.dot(weight.astype(jnp.bfloat16), value, preferred_element_type=jnp.float32)
         part_out[i] = (acc * (1.0 / total)).astype(jnp.bfloat16)
         lse = jnp.broadcast_to(top + jnp.log(total), (rows, HEAD_DIM))
-        lse_out[i] = jnp.transpose(lse)[:8]
+        lse_out[i] = jnp.transpose(lse)[:1]
 
     def mask_for(ids):
         asker = column(ids[...])[:, :1]
@@ -716,9 +716,9 @@
             pltpu.VMEM((deepest, PIECES, depth, HEAD_DIM), jnp.bfloat16),
             asked,
             asked,
-            pltpu.VMEM((heads, 8, rows), jnp.float32),
+            pltpu.VMEM((heads, 1, rows), jnp.float32),
             asked,
-            pltpu.VMEM((heads, 8, rows), jnp.float32),
+            pltpu.VMEM((heads, 1, rows), jnp.float32),
             ids,
             ids,
             ids,

time: 29.4 us -> 29.4 us (level)
  no operation moved by 1% of the time
where the time goes in v6:
time: 29.4 us; the launch traced here: 29.2 us
  Pallas kernels  29.2 us (99%)
    pallas_call x1, Pallas kernels, on_device(): pl.pallas_call(functools.partial(kernel, n, heads, rows), out_shape=(pltp...  28.3 us
    pallas_call x1, Pallas kernels, on_device(): pl.pallas_call(functools.partial(blend, heads), out_shape=jax.ShapeDtypeS...  0.88 us

profile of v6, /device:TPU:9, one launch (start us, length us, event | category | flops | bytes accessed | tf_op | source)
XLA Modules:
  0.0 29.2 jit_solution(12108756765406927612)
XLA Ops:
  0.0 0.0 copy-start
  0.0 28.3 %shard_map.64 = (bf16[8,256,128]{2,1,0:T(8,128)(2,1)S(1)}, f32[256,128]{1,0:T(8,128)S(1)}, s32[256,128]{1,0:T(8,128)S(1)}) custom-call(bf16[256,1024]{1,0:T(8,128)(2,1)} %q_hbm.1, bf16[256,1024]{1,0:T(8,128)(2,1)} %k_hbm.1, bf16[256,1024]{1,0:T(8,128)(2,1)} %v_hbm.1, s32[1,256]{1,0:T(1,128)} %bitcast.2, s32[1,256]{1,0:T(1,128)} %bitcast.3), custom_call_target="tpu_custom_call" | custom-call | tf_op jit(solution)/shard_map/pallas_call | solution.py:702
  28.3 0.0 copy-done
  28.3 0.9 %shard_map.65 = bf16[256,1024]{1,0:T(8,128)(2,1)} custom-call(bf16[8,256,128]{2,1,0:T(8,128)(2,1)S(1)} %get-tuple-element.8.att, f32[256,128]{1,0:T(8,128)S(1)} %get-tuple-element.9.inverse_ref, s32[256,128]{1,0:T(8,128)S(1)} %get-tuple-element.10.image_ref, f32[2,1024]{1,0:T(2,128)S(1)} %copy-done), custom_call_target="tpu_custom_call" | custom-call | tf_op jit(solution)/shard_map/pallas_call | solution.py:754
Async XLA Ops:
  0.0 28.3 %copy-start = (f32[2,1024]{1,0:T(2,128)S(1)}, f32[2,1024]{1,0:T(2,128)}, u32[]{:S(2)}) copy-start(f32[2,1024]{1,0:T(2,128)} %gain_ref.1) | copy-start | bytes 24580
